TPU v7x, 32 devices: a whole 2x2x4 slice. The times are simulated.
32 devices in a mesh: sub: 16 (over z, y, x), agg: 2 (over core).
Axes of the slice: x: 2, y: 2, z: 4, core: 2. Of those that a mesh axis runs over, the one named last changes fastest.
Arguments:
- block_values: float32 [7, 4, 4, 32768], P(None, None, None, ('sub', 'agg'))
- block_cols: int32 [7, 32768], P(None, ('sub', 'agg')), may hold values from 0 to 32767, as said below
- coarse_rhs: float32 [4, 32768], P(None, ('sub', 'agg'))
- guess: float32 [4, 32768], P(None, ('sub', 'agg')), may hold values from -3 to 3
- bound_low: int32 [1], replicated, may hold values from 20 to 26
- bound_high: int32 [1], replicated, may hold values from 32 to 40
Outputs:
- smoothed: float32 [4, 32768], P(None, ('sub', 'agg'))
- residual: float32 [4, 32768], P(None, ('sub', 'agg'))
- residual_rms: float32 [1], replicated
Inputs may be any that keep to these rules, and one draw needn't show every extreme that they name: Block rows form 32768 / 1024 planes of 1024 consecutive rows, in a periodic order. block_cols[0] is the row itself, block_cols[1] a row of the previous plane, block_cols[2] a row of the next plane, block_cols[3] to block_cols[6] rows of the same plane.
All inputs are finite; a program needn't handle non-finite values.
Results may differ from a plain program's by a relative error of at most 0.0001.
Values sent between devices are 32-bit elements; how exact they have to be, the bound alone decides.
A program may use at most 64 MiB of HBM per device.

v0:
```python
import functools

import jax
import jax.numpy as jnp
from jax import lax
from jax.experimental import pallas as pl
from jax.experimental.pallas import tpu as pltpu
from jax.sharding import PartitionSpec as P

STEPS = 4
ONE_ROUND = 32
LANES = 128
MESH = pl.DeviceIdType.MESH


def gather_lanes(rows, index):
    return jnp.take_along_axis(rows, index, axis=1, mode="promise_in_bounds")


def kernel(
    subs, aggs, shape,
    values_hbm, cols_hbm, rhs_hbm, guess_hbm, low_ref, high_ref,
    smoothed_out, residual_out, rms_ref,
    values, cols, cols_flat, rhs, field, beside, lane_of, tile_of, coef,
    near_sums, far_sums,
    values_sem, load_sem, send_sem, recv_sem,
    near_send, near_recv, far_send, far_recv,
):
    blocks, comp, tiles = shape
    devices = subs * aggs
    rows = tiles * LANES
    load_cols = pltpu.make_async_copy(cols_hbm, cols, load_sem.at[0])
    load_guess = pltpu.make_async_copy(guess_hbm, field.at[0], load_sem.at[1])
    load_rhs = pltpu.make_async_copy(rhs_hbm, rhs, load_sem.at[2])
    for load in (load_guess, load_cols):
        load.start()
    own = [0] + list(range(3, blocks))
    per_block = comp * comp * tiles

    def load_values(k):
        part = pl.ds(k * per_block, per_block)
        return pltpu.make_async_copy(values_hbm.at[part], values.at[part], values_sem.at[k])

    for k in own + [1, 2]:
        load_values(k).start()
    load_rhs.start()

    sub, agg = lax.axis_index("sub"), lax.axis_index("agg")
    me = sub * aggs + agg

    def ahead_of(place, by, size):
        to = place + by
        return jnp.where(to >= size, to - size, to)

    def beside_me(by_sub, by_agg):
        return (ahead_of(sub, by_sub, subs), ahead_of(agg, by_agg, aggs))

    def ring(way):
        turn = jnp.where(way == 0, agg == aggs - 1, agg == 0)
        to_sub = jnp.where(way == 0, ahead_of(sub, 1, subs), ahead_of(sub, subs - 1, subs))
        to_agg = jnp.where(way == 0, ahead_of(agg, 1, aggs), ahead_of(agg, aggs - 1, aggs))
        return (jnp.where(turn, to_sub, sub), to_agg)

    following = ahead_of(me, 1, devices)
    previous = ahead_of(me, devices - 1, devices)
    one_round = devices <= ONE_ROUND
    if one_round:
        near_steps = [(a, b) for a in range(subs) for b in range(aggs)][1:]
        near_steps = near_steps[::-1]
        near, near_me = devices, me
        far_steps = []
    else:
        near_steps = [(0, b) for b in range(1, aggs)]
        near, near_me = aggs, agg
        far_steps = [(a, 0) for a in range(1, subs)]
    near_partners = [beside_me(a, b) for a, b in near_steps]
    far_partners = [beside_me(a, b) for a, b in far_steps]

    barrier = pltpu.get_barrier_semaphore()
    partners = far_partners + near_partners
    if not one_round:
        partners = [ring(0), ring(1)] + partners
    for partner in partners:
        pl.semaphore_signal(barrier, inc=1, device_id=partner, device_id_type=MESH)

    load_guess.wait()
    pl.semaphore_wait(barrier, len(partners))

    def send(step, source, way):
        return pltpu.make_async_remote_copy(
            src_ref=source,
            dst_ref=beside.at[step, way],
            send_sem=send_sem.at[step, way],
            recv_sem=recv_sem.at[step, way],
            device_id=ring(way),
            device_id_type=MESH,
        )

    for way in range(2):
        send(0, field.at[0], way).start()

    low = jnp.full((tiles, LANES), low_ref[0], jnp.int32).astype(jnp.float32) / 4.0
    high = jnp.full((tiles, LANES), high_ref[0], jnp.int32).astype(jnp.float32) / 4.0
    centre = (high + low) / 2.0
    half = (high - low) / 2.0
    spread = centre / half
    ratio = 1.0 / spread
    coef[0, 0] = jnp.zeros((tiles, LANES), jnp.float32)
    coef[0, 1] = 1.0 / centre
    for t in range(1, STEPS):
        ahead = 1.0 / (2.0 * spread - ratio)
        coef[t, 0] = ahead * ratio
        coef[t, 1] = 2.0 * ahead / half
        ratio = ahead

    load_cols.wait()
    for c in range(tiles):
        cols_flat[pl.ds(c * 8, blocks), :] = cols[:, c * LANES:(c + 1) * LANES]
    for k in range(1, blocks):
        plane = {1: previous, 2: following}.get(k, me)
        local = cols_flat[pl.ds(k, tiles, stride=8), :] - plane * rows
        lane_of[k] = local & (LANES - 1)
        tile_of[k] = local >> 7

    def taken(source, k):
        lanes, tile = lane_of[k], tile_of[k]
        out = [None] * comp
        for r in range(tiles):
            here = tile == r
            for j in range(comp):
                row = jnp.broadcast_to(source[pl.ds(r * comp + j, 1), :], (tiles, LANES))
                got = gather_lanes(row, lanes)
                out[j] = got if r == 0 else jnp.where(here, got, out[j])
        return out

    def combine(k, got, total):
        total = list(total)
        for i in range(comp):
            base = (k * comp + i) * comp * tiles
            for j in range(comp):
                total[i] = total[i] - values[pl.ds(base + j, tiles, stride=comp), :] * got[j]
        return total

    def own_part(t, residual):
        source = field.at[t]
        direct = [source[pl.ds(j, tiles, stride=comp), :] for j in range(comp)]
        residual = combine(0, direct, residual)
        for k in own[1:]:
            residual = combine(k, taken(source, k), residual)
        return direct, residual

    def far_part(t, residual):
        even = 1 - lax.rem(me, 2)
        for way in (even, 1 - even):
            send(t, field.at[t], way).wait_recv()
            residual = combine(1 + way, taken(beside.at[t, way], 1 + way), residual)
        return residual

    load_rhs.wait()
    for k in own + [1, 2]:
        load_values(k).wait()

    def step(t, carry):
        smoothed, residual = carry
        direct, residual = own_part(t, residual)
        smoothed = [s + d for s, d in zip(smoothed, direct)]
        residual = far_part(t, residual)
        for j in range(comp):
            field[t + 1, pl.ds(j, tiles, stride=comp), :] = (
                coef[t, 0] * direct[j] + coef[t, 1] * residual[j]
            )
        for way in range(2):
            send(t + 1, field.at[t + 1], way).start()
        return smoothed, residual

    smoothed = [jnp.zeros((tiles, LANES), jnp.float32) for j in range(comp)]
    residual = [rhs[pl.ds(j, tiles, stride=comp), :] for j in range(comp)]
    smoothed, residual = lax.fori_loop(0, STEPS, step, (smoothed, residual))

    direct, residual = own_part(STEPS, residual)
    for j in range(comp):
        smoothed_out[pl.ds(j, tiles, stride=comp), :] = smoothed[j] + direct[j]
    residual = far_part(STEPS, residual)

    squares = residual[0] * residual[0]
    for j in range(1, comp):
        squares = squares + residual[j] * residual[j]
    partial = jnp.sum(squares, axis=0, keepdims=True)

    def spread_sums(sums, slot, partner, send_sems, recv_sems, d):
        return pltpu.make_async_remote_copy(
            src_ref=sums.at[slot],
            dst_ref=sums.at[slot],
            send_sem=send_sems.at[d],
            recv_sem=recv_sems.at[slot],
            device_id=partner,
            device_id_type=MESH,
        )

    def slot_of(partner):
        return partner[0] * aggs + partner[1] if one_round else partner[1]

    near_sums[near_me] = partial
    for d, partner in enumerate(near_partners):
        spread_sums(near_sums, near_me, partner, near_send, near_recv, d).start()
    for j in range(comp):
        residual_out[pl.ds(j, tiles, stride=comp), :] = residual[j]
    for d, partner in enumerate(near_partners):
        spread_sums(near_sums, slot_of(partner), partner, near_send, near_recv, d).wait_recv()
    total = jnp.sum(near_sums[...], axis=0)
    if far_partners:
        far_sums[sub] = total
        for d, partner in enumerate(far_partners):
            spread_sums(far_sums, sub, partner, far_send, far_recv, d).start()
        for d, partner in enumerate(far_partners):
            spread_sums(far_sums, partner[0], partner, far_send, far_recv, d).wait_recv()
        total = jnp.sum(far_sums[...], axis=0)
    count = float(comp * rows * devices)
    rms_ref[...] = jnp.sqrt(jnp.sum(total, axis=1, keepdims=True) / count + 1e-06)

    for t in range(STEPS + 1):
        for way in range(2):
            send(t, field.at[t], way).wait_send()
    for d, partner in enumerate(near_partners):
        spread_sums(near_sums, near_me, partner, near_send, near_recv, d).wait_send()
    for d, partner in enumerate(far_partners):
        spread_sums(far_sums, sub, partner, far_send, far_recv, d).wait_send()


def put_out(*refs):
    count = len(refs) // 2
    sems = refs[-1]
    copies = [
        pltpu.make_async_copy(refs[i], refs[count + i], sems.at[i]) for i in range(count)
    ]
    for copy in copies:
        copy.start()
    for copy in copies:
        copy.wait()


def flat(field, tiles):
    comp = field.shape[-2]
    lead = field.shape[:-2]
    cut = field.reshape(lead + (comp, tiles, LANES))
    return jnp.swapaxes(cut, -3, -2).reshape(-1, LANES)


def unflat(field, comp):
    tiles = field.shape[0] // comp
    return jnp.swapaxes(field.reshape(tiles, comp, LANES), 0, 1).reshape(comp, tiles * LANES)


def shards(subs, aggs, block_values, block_cols, coarse_rhs, guess, bound_low, bound_high):
    blocks, comp, _, rows = block_values.shape
    tiles = rows // LANES
    devices = subs * aggs
    near, far = (devices, 1) if devices <= ONE_ROUND else (aggs, subs)
    f32 = jnp.float32
    plane = (tiles * comp, LANES)
    anywhere = pl.BlockSpec(memory_space=pl.ANY)
    in_vmem = pl.BlockSpec(memory_space=pltpu.VMEM)
    in_hbm = pl.BlockSpec(memory_space=pltpu.HBM)
    dma = pltpu.SemaphoreType.DMA
    smoothed, residual, rms = pl.pallas_call(
        functools.partial(kernel, subs, aggs, (blocks, comp, tiles)),
        out_shape=(
            jax.ShapeDtypeStruct(plane, f32),
            jax.ShapeDtypeStruct(plane, f32),
            jax.ShapeDtypeStruct((1, 1), f32),
        ),
        in_specs=[in_hbm] * 4 + [pl.BlockSpec(memory_space=pltpu.SMEM)] * 2,
        out_specs=(in_vmem,) * 3,
        scratch_shapes=[
            pltpu.VMEM((blocks * comp * comp * tiles, LANES), f32),
            pltpu.VMEM((blocks, rows), jnp.int32),
            pltpu.VMEM((8 * tiles, LANES), jnp.int32),
            pltpu.VMEM(plane, f32),
            pltpu.VMEM((STEPS + 1,) + plane, f32),
            pltpu.VMEM((STEPS + 1, 2) + plane, f32),
            pltpu.VMEM((blocks, tiles, LANES), jnp.int32),
            pltpu.VMEM((blocks, tiles, LANES), jnp.int32),
            pltpu.VMEM((STEPS, 2, tiles, LANES), f32),
            pltpu.VMEM((near, 1, LANES), f32),
            pltpu.VMEM((far, 1, LANES), f32),
            dma((blocks,)),
            dma((5,)),
            dma((STEPS + 1, 2)),
            dma((STEPS + 1, 2)),
            dma((max(near - 1, 1),)),
            dma((near,)),
            dma((max(far - 1, 1),)),
            dma((far,)),
        ],
        compiler_params=pltpu.CompilerParams(collective_id=0, has_side_effects=True, vmem_limit_bytes=8 * 1024 * 1024),
    )(
        *[
            pltpu.with_memory_space_constraint(x, pltpu.HBM)
            for x in (
                flat(block_values, tiles), block_cols, flat(coarse_rhs, tiles), flat(guess, tiles),
            )
        ],
        bound_low, bound_high,
    )
    smoothed, residual, rms = pl.pallas_call(
        put_out,
        out_shape=(
            jax.ShapeDtypeStruct(plane, f32),
            jax.ShapeDtypeStruct(plane, f32),
            jax.ShapeDtypeStruct((1, 1), f32),
        ),
        in_specs=[anywhere] * 3,
        out_specs=(anywhere,) * 3,
        scratch_shapes=[dma((3,))],
        compiler_params=pltpu.CompilerParams(vmem_limit_bytes=8 * 1024 * 1024),
    )(smoothed, residual, rms)
    return unflat(smoothed, comp), unflat(residual, comp), rms.reshape(1)


def solution(mesh):
    split = ("sub", "agg")
    return jax.shard_map(
        functools.partial(shards, mesh.shape["sub"], mesh.shape["agg"]),
        mesh=mesh,
        in_specs=(
            P(None, None, None, split),
            P(None, split),
            P(None, split),
            P(None, split),
            P(),
            P(),
        ),
        out_specs=(P(None, split), P(None, split), P()),
        check_vma=False,
    )
```

profile of v0, /device:TPU:0, one launch (start us, length us, event | category | flops | bytes accessed | tf_op | source)
XLA Modules:
  0.0 37.1 jit_solution(9613253675432601830)
XLA Ops:
  1.9 33.9 %shard_map.85 = (f32[32,128]{1,0:T(8,128)S(1)}, f32[32,128]{1,0:T(8,128)S(1)}, f32[1,1]{1,0:T(1,128)}) custom-call(f32[896,128]{1,0:T(8,128)} %bitcast.26, s32[7,1024]{1,0:T(8,128)} %cols_hbm.1, f32[32,128]{1,0:T(8,128)} %bitcast.27, f32[32,128]{1,0:T(8,128)} %bitcast.28, s32[1]{0:T(128)S(6)} %copy.14.low_ref, s32[1]{0:T(128)S(6)} %copy.15.high_ref), custom_call_target="tpu_custom_call" | custom-call | tf_op jit(solution)/shard_map/pallas_call | solution.py:265
  35.8 1.3 %shard_map.86 = (f32[32,128]{1,0:T(8,128)}, f32[32,128]{1,0:T(8,128)}, f32[1,1]{1,0:T(1,128)}) custom-call(f32[32,128]{1,0:T(8,128)S(1)} %get-tuple-element.9.refs_0_, f32[32,128]{1,0:T(8,128)S(1)} %get-tuple-element.10.refs_1_, f32[1,1]{1,0:T(1,128)} %get-tuple-element.11.refs_2_), custom_call_target="tpu_custom_call" | custom-call | tf_op jit(solution)/shard_map/pallas_call | solution.py:305
where the time goes:
time: 37.3 us; the launch traced here: 37.1 us
  Pallas kernels  35.1 us (94%)
  between operations  1.93 us (5%)
    pallas_call x1, Pallas kernels, shards(): pl.pallas_call(functools.partial(kernel, subs, aggs, (blocks, comp, tiles...  33.9 us
    pallas_call x1, Pallas kernels, shards(): pl.pallas_call(put_out, out_shape=(jax.ShapeDtypeStruct(plane, f32), jax....  1.27 us

commit v1 on v0

--- a/solution.py
+++ b/solution.py
@@ -216,7 +216,7 @@
             spread_sums(far_sums, partner[0], partner, far_send, far_recv, d).wait_recv()
         total = jnp.sum(far_sums[...], axis=0)
     count = float(comp * rows * devices)
-    rms_ref[...] = jnp.sqrt(jnp.sum(total, axis=1, keepdims=True) / count + 1e-06)
+    rms_ref[...] = jnp.broadcast_to(jnp.sqrt(jnp.sum(total, axis=1, keepdims=True) / count + 1e-06), rms_ref.shape)
 
     for t in range(STEPS + 1):
         for way in range(2):
@@ -231,7 +231,7 @@
     count = len(refs) // 2
     sems = refs[-1]
     copies = [
-        pltpu.make_async_copy(refs[i], refs[count + i], sems.at[i]) for i in range(count)
+        pltpu.make_async_copy(refs[i] if i < 2 else refs[i].at[pl.ds(0, 1)], refs[count + i], sems.at[i]) for i in range(count)
     ]
     for copy in copies:
         copy.start()
@@ -267,7 +267,7 @@
         out_shape=(
             jax.ShapeDtypeStruct(plane, f32),
             jax.ShapeDtypeStruct(plane, f32),
-            jax.ShapeDtypeStruct((1, 1), f32),
+            jax.ShapeDtypeStruct((8, LANES), f32),
         ),
         in_specs=[in_hbm] * 4 + [pl.BlockSpec(memory_space=pltpu.SMEM)] * 2,
         out_specs=(in_vmem,) * 3,
@@ -307,14 +307,14 @@
         out_shape=(
             jax.ShapeDtypeStruct(plane, f32),
             jax.ShapeDtypeStruct(plane, f32),
-            jax.ShapeDtypeStruct((1, 1), f32),
+            jax.ShapeDtypeStruct((1, LANES), f32),
         ),
         in_specs=[anywhere] * 3,
         out_specs=(anywhere,) * 3,
         scratch_shapes=[dma((3,))],
         compiler_params=pltpu.CompilerParams(vmem_limit_bytes=8 * 1024 * 1024),
     )(smoothed, residual, rms)
-    return unflat(smoothed, comp), unflat(residual, comp), rms.reshape(1)
+    return unflat(smoothed, comp), unflat(residual, comp), rms[0,:1]
 
 
 def solution(mesh):

time: 37.3 us -> 36.1 us (0.968)
  Pallas kernels: 35.1 us -> 34 us
    pallas_call x1, Pallas kernels: 1.27 us -> 0.64 us  [shards(): pl.pallas_call(put_out, out_shape=(jax.ShapeDtypeStruct(plane, f32), jax....]
    pallas_call x1, Pallas kernels: 33.9 us -> 33.3 us  [shards(): pl.pallas_call(functools.partial(kernel, subs, aggs, (blocks, comp, tiles...]
where the time goes in v1:
time: 36.1 us; the launch traced here: 35.9 us
  Pallas kernels  34 us (94%)
  between operations  1.93 us (5%)
    pallas_call x1, Pallas kernels, shards(): pl.pallas_call(functools.partial(kernel, subs, aggs, (blocks, comp, tiles...  33.3 us

profile of v1, /device:TPU:0, one launch (start us, length us, event | category | flops | bytes accessed | tf_op | source)
XLA Modules:
  0.0 35.9 jit_solution(3584242463116175048)
XLA Ops:
  1.9 33.3 %shard_map.85 = (f32[32,128]{1,0:T(8,128)S(1)}, f32[32,128]{1,0:T(8,128)S(1)}, f32[8,128]{1,0:T(8,128)S(1)}) custom-call(f32[896,128]{1,0:T(8,128)} %bitcast.27, s32[7,1024]{1,0:T(8,128)} %cols_hbm.1, f32[32,128]{1,0:T(8,128)} %bitcast.28, f32[32,128]{1,0:T(8,128)} %bitcast.29, s32[1]{0:T(128)S(6)} %copy.14.low_ref, s32[1]{0:T(128)S(6)} %copy.15.high_ref), custom_call_target="tpu_custom_call" | custom-call | tf_op jit(solution)/shard_map/pallas_call | solution.py:265
  35.3 0.6 %shard_map.86 = (f32[32,128]{1,0:T(8,128)}, f32[32,128]{1,0:T(8,128)}, f32[1,128]{1,0:T(1,128)}) custom-call(f32[32,128]{1,0:T(8,128)S(1)} %get-tuple-element.9.refs_0_, f32[32,128]{1,0:T(8,128)S(1)} %get-tuple-element.10.refs_1_, f32[8,128]{1,0:T(8,128)S(1)} %get-tuple-element.11.refs_2_), custom_call_target="tpu_custom_call" | custom-call | tf_op jit(solution)/shard_map/pallas_call | solution.py:305

commit v2 on v1

--- a/solution.py
+++ b/solution.py
@@ -9,6 +9,7 @@
 
 STEPS = 4
 ONE_ROUND = 32
+GHOSTS = 1
 LANES = 128
 MESH = pl.DeviceIdType.MESH
 
@@ -23,8 +24,10 @@
     smoothed_out, residual_out, rms_ref,
     values, cols, cols_flat, rhs, field, beside, lane_of, tile_of, coef,
     near_sums, far_sums,
+    ghost_values, ghost_cols, ghost_flat, ghost_lane, ghost_tile, ghost_residual, beyond,
     values_sem, load_sem, send_sem, recv_sem,
     near_send, near_recv, far_send, far_recv,
+    ghost_send, ghost_recv, beyond_send, beyond_recv,
 ):
     blocks, comp, tiles = shape
     devices = subs * aggs
@@ -76,6 +79,21 @@
     near_partners = [beside_me(a, b) for a, b in near_steps]
     far_partners = [beside_me(a, b) for a, b in far_steps]
 
+    ghosts = GHOSTS if one_round and devices % (2 * GHOSTS) == 0 else 0
+    even = 1 - lax.rem(me, 2)
+    across = 1 - even
+
+    def has_ghost(border):
+        return lax.rem(border + 1, devices // ghosts) == 0
+
+    if ghosts:
+        inner = jnp.where(even == 1, following, previous)
+        outer = jnp.where(even == 1, previous, following)
+        own_ghost = has_ghost(jnp.where(even == 1, previous, me))
+        feeds = has_ghost(jnp.where(even == 1, following, ahead_of(me, devices - 2, devices)))
+        second = jnp.where(even == 1, ahead_of(me, 2, devices), ahead_of(me, devices - 2, devices))
+        fed = (second // aggs, lax.rem(second, aggs))
+
     barrier = pltpu.get_barrier_semaphore()
     partners = far_partners + near_partners
     if not one_round:
@@ -98,6 +116,35 @@
 
     for way in range(2):
         send(0, field.at[0], way).start()
+
+    def feed(t):
+        return pltpu.make_async_remote_copy(
+            src_ref=field.at[t],
+            dst_ref=beyond.at[t],
+            send_sem=beyond_send.at[t],
+            recv_sem=beyond_recv.at[t],
+            device_id=fed,
+            device_id_type=MESH,
+        )
+
+    def give(k):
+        source, target = cols, ghost_cols
+        if k < blocks:
+            part = pl.ds(k * per_block, per_block)
+            source, target = values.at[part], ghost_values.at[part]
+        return pltpu.make_async_remote_copy(
+            src_ref=source,
+            dst_ref=target,
+            send_sem=ghost_send.at[k],
+            recv_sem=ghost_recv.at[k],
+            device_id=ring(even),
+            device_id_type=MESH,
+        )
+
+    def crosses(t, way):
+        if not ghosts:
+            return True
+        return jnp.logical_not(own_ghost & (way == across) & (t >= 2))
 
     low = jnp.full((tiles, LANES), low_ref[0], jnp.int32).astype(jnp.float32) / 4.0
     high = jnp.full((tiles, LANES), high_ref[0], jnp.int32).astype(jnp.float32) / 4.0
@@ -113,16 +160,19 @@
         coef[t, 1] = 2.0 * ahead / half
         ratio = ahead
 
+    def index(cols, cols_flat, lane_of, tile_of, before, here, after):
+        for c in range(tiles):
+            cols_flat[pl.ds(c * 8, blocks), :] = cols[:, c * LANES:(c + 1) * LANES]
+        for k in range(1, blocks):
+            plane = {1: before, 2: after}.get(k, here)
+            local = cols_flat[pl.ds(k, tiles, stride=8), :] - plane * rows
+            lane_of[k] = local & (LANES - 1)
+            tile_of[k] = local >> 7
+
     load_cols.wait()
-    for c in range(tiles):
-        cols_flat[pl.ds(c * 8, blocks), :] = cols[:, c * LANES:(c + 1) * LANES]
-    for k in range(1, blocks):
-        plane = {1: previous, 2: following}.get(k, me)
-        local = cols_flat[pl.ds(k, tiles, stride=8), :] - plane * rows
-        lane_of[k] = local & (LANES - 1)
-        tile_of[k] = local >> 7
-
-    def taken(source, k):
+    index(cols, cols_flat, lane_of, tile_of, previous, me, following)
+
+    def taken(source, k, lane_of=lane_of, tile_of=tile_of):
         lanes, tile = lane_of[k], tile_of[k]
         out = [None] * comp
         for r in range(tiles):
@@ -133,7 +183,7 @@
                 out[j] = got if r == 0 else jnp.where(here, got, out[j])
         return out
 
-    def combine(k, got, total):
+    def combine(k, got, total, values=values):
         total = list(total)
         for i in range(comp):
             base = (k * comp + i) * comp * tiles
@@ -150,15 +200,53 @@
         return direct, residual
 
     def far_part(t, residual):
-        even = 1 - lax.rem(me, 2)
-        for way in (even, 1 - even):
-            send(t, field.at[t], way).wait_recv()
+        for way in (even, across):
+            @pl.when(crosses(t, way))
+            def _():
+                send(t, field.at[t], way).wait_recv()
             residual = combine(1 + way, taken(beside.at[t, way], 1 + way), residual)
         return residual
 
     load_rhs.wait()
     for k in own + [1, 2]:
         load_values(k).wait()
+
+    if ghosts:
+        ghost_residual[...] = jnp.zeros(ghost_residual.shape, jnp.float32)
+
+        @pl.when(own_ghost)
+        def _():
+            for k in [blocks] + own + [1, 2]:
+                give(k).start()
+
+    def ghost_step(t):
+        @pl.when(t == 1)
+        def _():
+            for k in [blocks] + own + [1, 2]:
+                give(k).wait_recv()
+            here, past = outer, jnp.where(even == 1, ahead_of(me, devices - 2, devices), ahead_of(me, 2, devices))
+            before = jnp.where(even == 1, past, me)
+            after = jnp.where(even == 1, me, past)
+            index(ghost_cols, ghost_flat, ghost_lane, ghost_tile, before, here, after)
+            for j in range(comp):
+                ghost_residual[j] = centre * beside[1, across, pl.ds(j, tiles, stride=comp), :]
+
+        source = beside.at[t, across]
+        direct = [source[pl.ds(j, tiles, stride=comp), :] for j in range(comp)]
+        total = [ghost_residual[j] for j in range(comp)]
+        total = combine(0, direct, total, ghost_values)
+        for k in own[1:]:
+            total = combine(k, taken(source, k, ghost_lane, ghost_tile), total, ghost_values)
+        k = 2 - across
+        total = combine(k, taken(field.at[t], k, ghost_lane, ghost_tile), total, ghost_values)
+        feed(t).wait_recv()
+        k = 1 + across
+        total = combine(k, taken(beyond.at[t], k, ghost_lane, ghost_tile), total, ghost_values)
+        for j in range(comp):
+            ghost_residual[j] = total[j]
+            beside[t + 1, across, pl.ds(j, tiles, stride=comp), :] = (
+                coef[t, 0] * direct[j] + coef[t, 1] * total[j]
+            )
 
     def step(t, carry):
         smoothed, residual = carry
@@ -170,7 +258,17 @@
                 coef[t, 0] * direct[j] + coef[t, 1] * residual[j]
             )
         for way in range(2):
-            send(t + 1, field.at[t + 1], way).start()
+            @pl.when(crosses(t + 1, 1 - way))
+            def _():
+                send(t + 1, field.at[t + 1], way).start()
+        if ghosts:
+            @pl.when(feeds & (t + 1 < STEPS))
+            def _():
+                feed(t + 1).start()
+
+            @pl.when(own_ghost & (t >= 1) & (t < STEPS))
+            def _():
+                ghost_step(t)
         return smoothed, residual
 
     smoothed = [jnp.zeros((tiles, LANES), jnp.float32) for j in range(comp)]
@@ -220,7 +318,19 @@
 
     for t in range(STEPS + 1):
         for way in range(2):
-            send(t, field.at[t], way).wait_send()
+            @pl.when(crosses(t, 1 - way))
+            def _():
+                send(t, field.at[t], way).wait_send()
+    if ghosts:
+        @pl.when(feeds)
+        def _():
+            for t in range(1, STEPS):
+                feed(t).wait_send()
+
+        @pl.when(own_ghost)
+        def _():
+            for k in range(blocks + 1):
+                give(k).wait_send()
     for d, partner in enumerate(near_partners):
         spread_sums(near_sums, near_me, partner, near_send, near_recv, d).wait_send()
     for d, partner in enumerate(far_partners):
@@ -283,6 +393,13 @@
             pltpu.VMEM((STEPS, 2, tiles, LANES), f32),
             pltpu.VMEM((near, 1, LANES), f32),
             pltpu.VMEM((far, 1, LANES), f32),
+            pltpu.VMEM((blocks * comp * comp * tiles, LANES), f32),
+            pltpu.VMEM((blocks, rows), jnp.int32),
+            pltpu.VMEM((8 * tiles, LANES), jnp.int32),
+            pltpu.VMEM((blocks, tiles, LANES), jnp.int32),
+            pltpu.VMEM((blocks, tiles, LANES), jnp.int32),
+            pltpu.VMEM((comp, tiles, LANES), f32),
+            pltpu.VMEM((STEPS + 1,) + plane, f32),
             dma((blocks,)),
             dma((5,)),
             dma((STEPS + 1, 2)),
@@ -291,6 +408,10 @@
             dma((near,)),
             dma((max(far - 1, 1),)),
             dma((far,)),
+            dma((blocks + 1,)),
+            dma((blocks + 1,)),
+            dma((STEPS + 1,)),
+            dma((STEPS + 1,)),
         ],
         compiler_params=pltpu.CompilerParams(collective_id=0, has_side_effects=True, vmem_limit_bytes=8 * 1024 * 1024),
     )(

time: 36.1 us -> 32.2 us (0.89)
  Pallas kernels: 34 us -> 30.1 us
    pallas_call x1, Pallas kernels: 33.3 us -> 29.5 us  [shards(): pl.pallas_call(functools.partial(kernel, subs, aggs, (blocks, comp, tiles...]
where the time goes in v2:
time: 32.2 us; the launch traced here: 32 us
  Pallas kernels  30.1 us (93%)
  between operations  1.93 us (6%)
    pallas_call x1, Pallas kernels, shards(): pl.pallas_call(functools.partial(kernel, subs, aggs, (blocks, comp, tiles...  29.5 us

profile of v2, /device:TPU:0, one launch (start us, length us, event | category | flops | bytes accessed | tf_op | source)
XLA Modules:
  0.0 32.0 jit_solution(4255961702356165120)
XLA Ops:
  1.9 29.5 %shard_map.85 = (f32[32,128]{1,0:T(8,128)S(1)}, f32[32,128]{1,0:T(8,128)S(1)}, f32[8,128]{1,0:T(8,128)S(1)}) custom-call(f32[896,128]{1,0:T(8,128)} %bitcast.27, s32[7,1024]{1,0:T(8,128)} %cols_hbm.1, f32[32,128]{1,0:T(8,128)} %bitcast.28, f32[32,128]{1,0:T(8,128)} %bitcast.29, s32[1]{0:T(128)S(6)} %copy.14.low_ref, s32[1]{0:T(128)S(6)} %copy.15.high_ref), custom_call_target="tpu_custom_call" | custom-call | tf_op jit(solution)/shard_map/pallas_call | solution.py:375
  31.4 0.6 %shard_map.86 = (f32[32,128]{1,0:T(8,128)}, f32[32,128]{1,0:T(8,128)}, f32[1,128]{1,0:T(1,128)}) custom-call(f32[32,128]{1,0:T(8,128)S(1)} %get-tuple-element.9.refs_0_, f32[32,128]{1,0:T(8,128)S(1)} %get-tuple-element.10.refs_1_, f32[8,128]{1,0:T(8,128)S(1)} %get-tuple-element.11.refs_2_), custom_call_target="tpu_custom_call" | custom-call | tf_op jit(solution)/shard_map/pallas_call | solution.py:426

commit v3 on v2

--- a/solution.py
+++ b/solution.py
@@ -9,7 +9,9 @@
 
 STEPS = 4
 ONE_ROUND = 32
-GHOSTS = 1
+GHOSTS = 4
+FIRST_EVEN = 3
+FIRST_ODD = 8
 LANES = 128
 MESH = pl.DeviceIdType.MESH
 
@@ -26,7 +28,7 @@
     near_sums, far_sums,
     ghost_values, ghost_cols, ghost_flat, ghost_lane, ghost_tile, ghost_residual, beyond,
     values_sem, load_sem, send_sem, recv_sem,
-    near_send, near_recv, far_send, far_recv,
+    near_sems, far_sems,
     ghost_send, ghost_recv, beyond_send, beyond_recv,
 ):
     blocks, comp, tiles = shape
@@ -69,7 +71,7 @@
     one_round = devices <= ONE_ROUND
     if one_round:
         near_steps = [(a, b) for a in range(subs) for b in range(aggs)][1:]
-        near_steps = near_steps[::-1]
+        near_steps.sort(key=lambda step: min(step[0], subs - step[0]))
         near, near_me = devices, me
         far_steps = []
     else:
@@ -141,6 +143,8 @@
             device_id_type=MESH,
         )
 
+    given = own + [1, 2, blocks]
+
     def crosses(t, way):
         if not ghosts:
             return True
@@ -214,15 +218,16 @@
     if ghosts:
         ghost_residual[...] = jnp.zeros(ghost_residual.shape, jnp.float32)
 
-        @pl.when(own_ghost)
-        def _():
-            for k in [blocks] + own + [1, 2]:
-                give(k).start()
+        for side, first in ((1, FIRST_EVEN), (0, FIRST_ODD)):
+            @pl.when(own_ghost & (even == side))
+            def _():
+                for k in given[:first]:
+                    give(k).start()
 
     def ghost_step(t):
         @pl.when(t == 1)
         def _():
-            for k in [blocks] + own + [1, 2]:
+            for k in given:
                 give(k).wait_recv()
             here, past = outer, jnp.where(even == 1, ahead_of(me, devices - 2, devices), ahead_of(me, 2, devices))
             before = jnp.where(even == 1, past, me)
@@ -262,6 +267,13 @@
             def _():
                 send(t + 1, field.at[t + 1], way).start()
         if ghosts:
+            for side, first in ((1, FIRST_EVEN), (0, FIRST_ODD)):
+                if first <= blocks:
+                    @pl.when(own_ghost & (even == side) & (t == 0))
+                    def _():
+                        for k in given[first:]:
+                            give(k).start()
+
             @pl.when(feeds & (t + 1 < STEPS))
             def _():
                 feed(t + 1).start()
@@ -285,56 +297,54 @@
         squares = squares + residual[j] * residual[j]
     partial = jnp.sum(squares, axis=0, keepdims=True)
 
-    def spread_sums(sums, slot, partner, send_sems, recv_sems, d):
+    def spread_sums(sums, slot, partner, sems):
         return pltpu.make_async_remote_copy(
             src_ref=sums.at[slot],
             dst_ref=sums.at[slot],
-            send_sem=send_sems.at[d],
-            recv_sem=recv_sems.at[slot],
+            send_sem=sems.at[0],
+            recv_sem=sems.at[1],
             device_id=partner,
             device_id_type=MESH,
         )
 
-    def slot_of(partner):
-        return partner[0] * aggs + partner[1] if one_round else partner[1]
+    def wait_sends():
+        for t in range(STEPS + 1):
+            for way in range(2):
+                @pl.when(crosses(t, 1 - way))
+                def _():
+                    send(t, field.at[t], way).wait_send()
+        if ghosts:
+            @pl.when(feeds)
+            def _():
+                for t in range(1, STEPS):
+                    feed(t).wait_send()
+
+            @pl.when(own_ghost)
+            def _():
+                for k in range(blocks + 1):
+                    give(k).wait_send()
 
     near_sums[near_me] = partial
-    for d, partner in enumerate(near_partners):
-        spread_sums(near_sums, near_me, partner, near_send, near_recv, d).start()
+    for partner in near_partners:
+        spread_sums(near_sums, near_me, partner, near_sems).start()
     for j in range(comp):
         residual_out[pl.ds(j, tiles, stride=comp), :] = residual[j]
-    for d, partner in enumerate(near_partners):
-        spread_sums(near_sums, slot_of(partner), partner, near_send, near_recv, d).wait_recv()
+    wait_sends()
+    if near_partners:
+        every = pl.ds(0, len(near_partners))
+        spread_sums(near_sums, every, near_partners[0], near_sems).wait_send()
+        spread_sums(near_sums, every, near_partners[0], near_sems).wait_recv()
     total = jnp.sum(near_sums[...], axis=0)
     if far_partners:
         far_sums[sub] = total
-        for d, partner in enumerate(far_partners):
-            spread_sums(far_sums, sub, partner, far_send, far_recv, d).start()
-        for d, partner in enumerate(far_partners):
-            spread_sums(far_sums, partner[0], partner, far_send, far_recv, d).wait_recv()
+        for partner in far_partners:
+            spread_sums(far_sums, sub, partner, far_sems).start()
+        every = pl.ds(0, len(far_partners))
+        spread_sums(far_sums, every, far_partners[0], far_sems).wait_send()
+        spread_sums(far_sums, every, far_partners[0], far_sems).wait_recv()
         total = jnp.sum(far_sums[...], axis=0)
     count = float(comp * rows * devices)
     rms_ref[...] = jnp.broadcast_to(jnp.sqrt(jnp.sum(total, axis=1, keepdims=True) / count + 1e-06), rms_ref.shape)
-
-    for t in range(STEPS + 1):
-        for way in range(2):
-            @pl.when(crosses(t, 1 - way))
-            def _():
-                send(t, field.at[t], way).wait_send()
-    if ghosts:
-        @pl.when(feeds)
-        def _():
-            for t in range(1, STEPS):
-                feed(t).wait_send()
-
-        @pl.when(own_ghost)
-        def _():
-            for k in range(blocks + 1):
-                give(k).wait_send()
-    for d, partner in enumerate(near_partners):
-        spread_sums(near_sums, near_me, partner, near_send, near_recv, d).wait_send()
-    for d, partner in enumerate(far_partners):
-        spread_sums(far_sums, sub, partner, far_send, far_recv, d).wait_send()
 
 
 def put_out(*refs):
@@ -404,10 +414,8 @@
             dma((5,)),
             dma((STEPS + 1, 2)),
             dma((STEPS + 1, 2)),
-            dma((max(near - 1, 1),)),
-            dma((near,)),
-            dma((max(far - 1, 1),)),
-            dma((far,)),
+            dma((2,)),
+            dma((2,)),
             dma((blocks + 1,)),
             dma((blocks + 1,)),
             dma((STEPS + 1,)),

time: 32.2 us -> 29.6 us (0.919)
  Pallas kernels: 30.1 us -> 27.5 us
    pallas_call x1, Pallas kernels: 29.5 us -> 26.9 us  [shards(): pl.pallas_call(functools.partial(kernel, subs, aggs, (blocks, comp, tiles...]
where the time goes in v3:
time: 29.6 us; the launch traced here: 29.5 us
  Pallas kernels  27.5 us (93%)
  between operations  1.93 us (7%)
    pallas_call x1, Pallas kernels, shards(): pl.pallas_call(functools.partial(kernel, subs, aggs, (blocks, comp, tiles...  26.9 us
    pallas_call x1, Pallas kernels, shards(): pl.pallas_call(put_out, out_shape=(jax.ShapeDtypeStruct(plane, f32), jax....  0.64 us

profile of v3, /device:TPU:0, one launch (start us, length us, event | category | flops | bytes accessed | tf_op | source)
XLA Modules:
  0.0 29.5 jit_solution(1547013063349731618)
XLA Ops:
  1.9 26.9 %shard_map.85 = (f32[32,128]{1,0:T(8,128)S(1)}, f32[32,128]{1,0:T(8,128)S(1)}, f32[8,128]{1,0:T(8,128)S(1)}) custom-call(f32[896,128]{1,0:T(8,128)} %bitcast.27, s32[7,1024]{1,0:T(8,128)} %cols_hbm.1, f32[32,128]{1,0:T(8,128)} %bitcast.28, f32[32,128]{1,0:T(8,128)} %bitcast.29, s32[1]{0:T(128)S(6)} %copy.14.low_ref, s32[1]{0:T(128)S(6)} %copy.15.high_ref), custom_call_target="tpu_custom_call" | custom-call | tf_op jit(solution)/shard_map/pallas_call | solution.py:385
  28.8 0.6 %shard_map.86 = (f32[32,128]{1,0:T(8,128)}, f32[32,128]{1,0:T(8,128)}, f32[1,128]{1,0:T(1,128)}) custom-call(f32[32,128]{1,0:T(8,128)S(1)} %get-tuple-element.9.refs_0_, f32[32,128]{1,0:T(8,128)S(1)} %get-tuple-element.10.refs_1_, f32[8,128]{1,0:T(8,128)S(1)} %get-tuple-element.11.refs_2_), custom_call_target="tpu_custom_call" | custom-call | tf_op jit(solution)/shard_map/pallas_call | solution.py:434

commit v4 on v1

--- a/solution.py
+++ b/solution.py
@@ -23,8 +23,10 @@
     smoothed_out, residual_out, rms_ref,
     values, cols, cols_flat, rhs, field, beside, lane_of, tile_of, coef,
     near_sums, far_sums,
+    ghost_values, ghost_lane, ghost_tile, part, ghost_part,
     values_sem, load_sem, send_sem, recv_sem,
-    near_send, near_recv, far_send, far_recv,
+    near_sems, far_sems,
+    ghost_send, ghost_recv, part_send, part_recv,
 ):
     blocks, comp, tiles = shape
     devices = subs * aggs
@@ -66,7 +68,7 @@
     one_round = devices <= ONE_ROUND
     if one_round:
         near_steps = [(a, b) for a in range(subs) for b in range(aggs)][1:]
-        near_steps = near_steps[::-1]
+        near_steps.sort(key=lambda step: min(step[0], subs - step[0]))
         near, near_me = devices, me
         far_steps = []
     else:
@@ -75,6 +77,9 @@
         far_steps = [(a, 0) for a in range(1, subs)]
     near_partners = [beside_me(a, b) for a, b in near_steps]
     far_partners = [beside_me(a, b) for a, b in far_steps]
+
+    even = 1 - lax.rem(me, 2)
+    across = 1 - even
 
     barrier = pltpu.get_barrier_semaphore()
     partners = far_partners + near_partners
@@ -98,6 +103,31 @@
 
     for way in range(2):
         send(0, field.at[0], way).start()
+
+    def give(i):
+        source, target = (
+            (values.at[pl.ds((1 + across) * per_block, per_block)], ghost_values),
+            (lane_of.at[1 + across], ghost_lane),
+            (tile_of.at[1 + across], ghost_tile),
+        )[i]
+        return pltpu.make_async_remote_copy(
+            src_ref=source,
+            dst_ref=target,
+            send_sem=ghost_send.at[i],
+            recv_sem=ghost_recv.at[i],
+            device_id=ring(even),
+            device_id_type=MESH,
+        )
+
+    def give_part(t):
+        return pltpu.make_async_remote_copy(
+            src_ref=part.at[t],
+            dst_ref=ghost_part.at[t],
+            send_sem=part_send.at[t],
+            recv_sem=part_recv.at[t],
+            device_id=ring(even),
+            device_id_type=MESH,
+        )
 
     low = jnp.full((tiles, LANES), low_ref[0], jnp.int32).astype(jnp.float32) / 4.0
     high = jnp.full((tiles, LANES), high_ref[0], jnp.int32).astype(jnp.float32) / 4.0
@@ -122,8 +152,7 @@
         lane_of[k] = local & (LANES - 1)
         tile_of[k] = local >> 7
 
-    def taken(source, k):
-        lanes, tile = lane_of[k], tile_of[k]
+    def taken(source, lanes, tile):
         out = [None] * comp
         for r in range(tiles):
             here = tile == r
@@ -133,7 +162,7 @@
                 out[j] = got if r == 0 else jnp.where(here, got, out[j])
         return out
 
-    def combine(k, got, total):
+    def combine(k, got, total, values=values):
         total = list(total)
         for i in range(comp):
             base = (k * comp + i) * comp * tiles
@@ -146,85 +175,122 @@
         direct = [source[pl.ds(j, tiles, stride=comp), :] for j in range(comp)]
         residual = combine(0, direct, residual)
         for k in own[1:]:
-            residual = combine(k, taken(source, k), residual)
+            residual = combine(k, taken(source, lane_of[k], tile_of[k]), residual)
         return direct, residual
 
-    def far_part(t, residual):
-        even = 1 - lax.rem(me, 2)
-        for way in (even, 1 - even):
-            send(t, field.at[t], way).wait_recv()
-            residual = combine(1 + way, taken(beside.at[t, way], 1 + way), residual)
-        return residual
-
-    load_rhs.wait()
-    for k in own + [1, 2]:
-        load_values(k).wait()
-
-    def step(t, carry):
-        smoothed, residual = carry
-        direct, residual = own_part(t, residual)
-        smoothed = [s + d for s, d in zip(smoothed, direct)]
-        residual = far_part(t, residual)
+    def far_part(t, way, residual):
+        k = 1 + way
+        return combine(k, taken(beside.at[t, way], lane_of[k], tile_of[k]), residual)
+
+    def arrive(t, way):
+        send(t, field.at[t], way).wait_recv()
+
+    def advance(t, direct, residual):
         for j in range(comp):
             field[t + 1, pl.ds(j, tiles, stride=comp), :] = (
                 coef[t, 0] * direct[j] + coef[t, 1] * residual[j]
             )
-        for way in range(2):
-            send(t + 1, field.at[t + 1], way).start()
+
+    load_rhs.wait()
+    for k in own + [1, 2]:
+        load_values(k).wait()
+    for i in range(3):
+        give(i).start()
+
+    def two_steps(pair, carry):
+        smoothed, residual = carry
+        t = 2 * pair
+        direct, residual = own_part(t, residual)
+        smoothed = [s + d for s, d in zip(smoothed, direct)]
+        arrive(t, even)
+        residual = far_part(t, even, residual)
+        for j in range(comp):
+            part[pair, pl.ds(j, tiles, stride=comp), :] = residual[j]
+        give_part(pair).start()
+        arrive(t, across)
+        residual = far_part(t, across, residual)
+        advance(t, direct, residual)
+        send(t + 1, field.at[t + 1], across).start()
+
+        direct, residual = own_part(t + 1, residual)
+        smoothed = [s + d for s, d in zip(smoothed, direct)]
+
+        @pl.when(pair == 0)
+        def _():
+            for i in range(3):
+                give(i).wait_recv()
+        give_part(pair).wait_recv()
+        other = [ghost_part[pair, pl.ds(j, tiles, stride=comp), :] for j in range(comp)]
+        other = combine(0, taken(field.at[t], ghost_lane[...], ghost_tile[...]), other, ghost_values)
+        for j in range(comp):
+            beside[t + 1, across, pl.ds(j, tiles, stride=comp), :] = (
+                coef[t, 0] * beside[t, across, pl.ds(j, tiles, stride=comp), :] + coef[t, 1] * other[j]
+            )
+        residual = far_part(t + 1, across, residual)
+        arrive(t + 1, even)
+        residual = far_part(t + 1, even, residual)
+        advance(t + 1, direct, residual)
+        for way in (even, across):
+            send(t + 2, field.at[t + 2], way).start()
         return smoothed, residual
 
     smoothed = [jnp.zeros((tiles, LANES), jnp.float32) for j in range(comp)]
     residual = [rhs[pl.ds(j, tiles, stride=comp), :] for j in range(comp)]
-    smoothed, residual = lax.fori_loop(0, STEPS, step, (smoothed, residual))
+    smoothed, residual = lax.fori_loop(0, STEPS // 2, two_steps, (smoothed, residual))
 
     direct, residual = own_part(STEPS, residual)
     for j in range(comp):
         smoothed_out[pl.ds(j, tiles, stride=comp), :] = smoothed[j] + direct[j]
-    residual = far_part(STEPS, residual)
+    for way in (even, across):
+        arrive(STEPS, way)
+        residual = far_part(STEPS, way, residual)
 
     squares = residual[0] * residual[0]
     for j in range(1, comp):
         squares = squares + residual[j] * residual[j]
     partial = jnp.sum(squares, axis=0, keepdims=True)
 
-    def spread_sums(sums, slot, partner, send_sems, recv_sems, d):
+    def spread_sums(sums, slot, partner, sems):
         return pltpu.make_async_remote_copy(
             src_ref=sums.at[slot],
             dst_ref=sums.at[slot],
-            send_sem=send_sems.at[d],
-            recv_sem=recv_sems.at[slot],
+            send_sem=sems.at[0],
+            recv_sem=sems.at[1],
             device_id=partner,
             device_id_type=MESH,
         )
 
-    def slot_of(partner):
-        return partner[0] * aggs + partner[1] if one_round else partner[1]
+    def wait_sends():
+        for t in range(STEPS + 1):
+            send(t, field.at[t], across).wait_send()
+            if t % 2 == 0:
+                send(t, field.at[t], even).wait_send()
+        for pair in range(STEPS // 2):
+            give_part(pair).wait_send()
+        for i in range(3):
+            give(i).wait_send()
 
     near_sums[near_me] = partial
-    for d, partner in enumerate(near_partners):
-        spread_sums(near_sums, near_me, partner, near_send, near_recv, d).start()
+    for partner in near_partners:
+        spread_sums(near_sums, near_me, partner, near_sems).start()
     for j in range(comp):
         residual_out[pl.ds(j, tiles, stride=comp), :] = residual[j]
-    for d, partner in enumerate(near_partners):
-        spread_sums(near_sums, slot_of(partner), partner, near_send, near_recv, d).wait_recv()
+    wait_sends()
+    if near_partners:
+        every = pl.ds(0, len(near_partners))
+        spread_sums(near_sums, every, near_partners[0], near_sems).wait_send()
+        spread_sums(near_sums, every, near_partners[0], near_sems).wait_recv()
     total = jnp.sum(near_sums[...], axis=0)
     if far_partners:
         far_sums[sub] = total
-        for d, partner in enumerate(far_partners):
-            spread_sums(far_sums, sub, partner, far_send, far_recv, d).start()
-        for d, partner in enumerate(far_partners):
-            spread_sums(far_sums, partner[0], partner, far_send, far_recv, d).wait_recv()
+        for partner in far_partners:
+            spread_sums(far_sums, sub, partner, far_sems).start()
+        every = pl.ds(0, len(far_partners))
+        spread_sums(far_sums, every, far_partners[0], far_sems).wait_send()
+        spread_sums(far_sums, every, far_partners[0], far_sems).wait_recv()
         total = jnp.sum(far_sums[...], axis=0)
     count = float(comp * rows * devices)
     rms_ref[...] = jnp.broadcast_to(jnp.sqrt(jnp.sum(total, axis=1, keepdims=True) / count + 1e-06), rms_ref.shape)
-
-    for t in range(STEPS + 1):
-        for way in range(2):
-            send(t, field.at[t], way).wait_send()
-    for d, partner in enumerate(near_partners):
-        spread_sums(near_sums, near_me, partner, near_send, near_recv, d).wait_send()
-    for d, partner in enumerate(far_partners):
-        spread_sums(far_sums, sub, partner, far_send, far_recv, d).wait_send()
 
 
 def put_out(*refs):
@@ -283,14 +349,21 @@
             pltpu.VMEM((STEPS, 2, tiles, LANES), f32),
             pltpu.VMEM((near, 1, LANES), f32),
             pltpu.VMEM((far, 1, LANES), f32),
+            pltpu.VMEM((comp * comp * tiles, LANES), f32),
+            pltpu.VMEM((tiles, LANES), jnp.int32),
+            pltpu.VMEM((tiles, LANES), jnp.int32),
+            pltpu.VMEM((STEPS // 2,) + plane, f32),
+            pltpu.VMEM((STEPS // 2,) + plane, f32),
             dma((blocks,)),
             dma((5,)),
             dma((STEPS + 1, 2)),
             dma((STEPS + 1, 2)),
-            dma((max(near - 1, 1),)),
-            dma((near,)),
-            dma((max(far - 1, 1),)),
-            dma((far,)),
+            dma((2,)),
+            dma((2,)),
+            dma((3,)),
+            dma((3,)),
+            dma((STEPS // 2,)),
+            dma((STEPS // 2,)),
         ],
         compiler_params=pltpu.CompilerParams(collective_id=0, has_side_effects=True, vmem_limit_bytes=8 * 1024 * 1024),
     )(

time: 36.1 us -> 29.1 us (0.81)
  Pallas kernels: 34 us -> 27 us
    pallas_call x1, Pallas kernels: 33.3 us -> 26.4 us  [shards(): pl.pallas_call(functools.partial(kernel, subs, aggs, (blocks, comp, tiles...]
where the time goes in v4:
time: 29.1 us; the launch traced here: 28.9 us
  Pallas kernels  27 us (93%)
  between operations  1.93 us (7%)
    pallas_call x1, Pallas kernels, shards(): pl.pallas_call(functools.partial(kernel, subs, aggs, (blocks, comp, tiles...  26.4 us
    pallas_call x1, Pallas kernels, shards(): pl.pallas_call(put_out, out_shape=(jax.ShapeDtypeStruct(plane, f32), jax....  0.64 us

profile of v4, /device:TPU:0, one launch (start us, length us, event | category | flops | bytes accessed | tf_op | source)
XLA Modules:
  0.0 28.9 jit_solution(3808130300533973455)
XLA Ops:
  1.9 26.4 %shard_map.85 = (f32[32,128]{1,0:T(8,128)S(1)}, f32[32,128]{1,0:T(8,128)S(1)}, f32[8,128]{1,0:T(8,128)S(1)}) custom-call(f32[896,128]{1,0:T(8,128)} %bitcast.27, s32[7,1024]{1,0:T(8,128)} %cols_hbm.1, f32[32,128]{1,0:T(8,128)} %bitcast.28, f32[32,128]{1,0:T(8,128)} %bitcast.29, s32[1]{0:T(128)S(6)} %copy.14.low_ref, s32[1]{0:T(128)S(6)} %copy.15.high_ref), custom_call_target="tpu_custom_call" | custom-call | tf_op jit(solution)/shard_map/pallas_call | solution.py:331
  28.3 0.6 %shard_map.86 = (f32[32,128]{1,0:T(8,128)}, f32[32,128]{1,0:T(8,128)}, f32[1,128]{1,0:T(1,128)}) custom-call(f32[32,128]{1,0:T(8,128)S(1)} %get-tuple-element.9.refs_0_, f32[32,128]{1,0:T(8,128)S(1)} %get-tuple-element.10.refs_1_, f32[8,128]{1,0:T(8,128)S(1)} %get-tuple-element.11.refs_2_), custom_call_target="tpu_custom_call" | custom-call | tf_op jit(solution)/shard_map/pallas_call | solution.py:378

commit v5 on v4

--- a/solution.py
+++ b/solution.py
@@ -21,12 +21,12 @@
     subs, aggs, shape,
     values_hbm, cols_hbm, rhs_hbm, guess_hbm, low_ref, high_ref,
     smoothed_out, residual_out, rms_ref,
-    values, cols, cols_flat, rhs, field, beside, lane_of, tile_of, coef,
+    values, cols, cols_flat, rhs, field, beside, local_of, coef,
     near_sums, far_sums,
-    ghost_values, ghost_lane, ghost_tile, part, ghost_part,
+    ghost_values, ghost_local, ghost_residual, beyond, part, ghost_part,
     values_sem, load_sem, send_sem, recv_sem,
     near_sems, far_sems,
-    ghost_send, ghost_recv, part_send, part_recv,
+    ghost_send, ghost_recv, part_send, part_recv, beyond_send, beyond_recv,
 ):
     blocks, comp, tiles = shape
     devices = subs * aggs
@@ -80,6 +80,8 @@
 
     even = 1 - lax.rem(me, 2)
     across = 1 - even
+    closing = one_round and devices >= 4
+    first, last, feeds = me == 0, me == devices - 1, me == 1
 
     barrier = pltpu.get_barrier_semaphore()
     partners = far_partners + near_partners
@@ -104,18 +106,53 @@
     for way in range(2):
         send(0, field.at[0], way).start()
 
-    def give(i):
-        source, target = (
-            (values.at[pl.ds((1 + across) * per_block, per_block)], ghost_values),
-            (lane_of.at[1 + across], ghost_lane),
-            (tile_of.at[1 + across], ghost_tile),
-        )[i]
+    def over(source, target, i):
         return pltpu.make_async_remote_copy(
             src_ref=source,
             dst_ref=target,
             send_sem=ghost_send.at[i],
             recv_sem=ghost_recv.at[i],
             device_id=ring(even),
+            device_id_type=MESH,
+        )
+
+    def give():
+        k = 1 + across
+        piece = pl.ds(k * per_block, per_block)
+        return [
+            over(values.at[piece], ghost_values.at[piece], 0),
+            over(local_of.at[k], ghost_local.at[k], 1),
+        ]
+
+    def give_rest(i):
+        k = 2 - across
+        if i == 0:
+            tail = pl.ds(3, blocks - 3)
+            return [
+                over(local_of.at[tail], ghost_local.at[tail], 2),
+                over(local_of.at[k], ghost_local.at[k], 3),
+            ]
+        block = k if i == 2 else own[max(i - 2, 0)]
+        piece = pl.ds(block * per_block, per_block)
+        return [over(values.at[piece], ghost_values.at[piece], 3 + i)]
+
+    pieces = blocks
+
+    def give_more(*which):
+        if closing and which:
+            @pl.when(first & which[0])
+            def _():
+                for i in which[1:]:
+                    for copy in give_rest(i):
+                        copy.start()
+
+    def feed(t):
+        return pltpu.make_async_remote_copy(
+            src_ref=field.at[t],
+            dst_ref=beyond.at[t],
+            send_sem=beyond_send.at[t],
+            recv_sem=beyond_recv.at[t],
+            device_id=((devices - 1) // aggs, (devices - 1) % aggs),
             device_id_type=MESH,
         )
 
@@ -148,11 +185,10 @@
         cols_flat[pl.ds(c * 8, blocks), :] = cols[:, c * LANES:(c + 1) * LANES]
     for k in range(1, blocks):
         plane = {1: previous, 2: following}.get(k, me)
-        local = cols_flat[pl.ds(k, tiles, stride=8), :] - plane * rows
-        lane_of[k] = local & (LANES - 1)
-        tile_of[k] = local >> 7
-
-    def taken(source, lanes, tile):
+        local_of[k] = cols_flat[pl.ds(k, tiles, stride=8), :] - plane * rows
+
+    def taken(source, local):
+        lanes, tile = local & (LANES - 1), local >> 7
         out = [None] * comp
         for r in range(tiles):
             here = tile == r
@@ -175,12 +211,12 @@
         direct = [source[pl.ds(j, tiles, stride=comp), :] for j in range(comp)]
         residual = combine(0, direct, residual)
         for k in own[1:]:
-            residual = combine(k, taken(source, lane_of[k], tile_of[k]), residual)
+            residual = combine(k, taken(source, local_of[k]), residual)
         return direct, residual
 
     def far_part(t, way, residual):
         k = 1 + way
-        return combine(k, taken(beside.at[t, way], lane_of[k], tile_of[k]), residual)
+        return combine(k, taken(beside.at[t, way], local_of[k]), residual)
 
     def arrive(t, way):
         send(t, field.at[t], way).wait_recv()
@@ -194,44 +230,78 @@
     load_rhs.wait()
     for k in own + [1, 2]:
         load_values(k).wait()
-    for i in range(3):
-        give(i).start()
+    for copy in give():
+        copy.start()
+
+    def foresee(t, total):
+        source = beside.at[t, across]
+        for j in range(comp):
+            ghost_residual[pl.ds(j, tiles, stride=comp), :] = total[j]
+            beside[t + 1, across, pl.ds(j, tiles, stride=comp), :] = (
+                coef[t, 0] * source[pl.ds(j, tiles, stride=comp), :] + coef[t, 1] * total[j]
+            )
+
+    def foresee_alone(t):
+        source = beside.at[t, across]
+        total = [ghost_residual[pl.ds(j, tiles, stride=comp), :] for j in range(comp)]
+        direct = [source[pl.ds(j, tiles, stride=comp), :] for j in range(comp)]
+        total = combine(0, direct, total, ghost_values)
+        for k in own[1:]:
+            total = combine(k, taken(source, ghost_local[k]), total, ghost_values)
+        k = 2 - across
+        total = combine(k, taken(field.at[t], ghost_local[k]), total, ghost_values)
+        feed(t).wait_recv()
+        k = 1 + across
+        total = combine(k, taken(beyond.at[t], ghost_local[k]), total, ghost_values)
+        foresee(t, total)
 
     def two_steps(pair, carry):
         smoothed, residual = carry
         t = 2 * pair
+        again = pair > 0
         direct, residual = own_part(t, residual)
         smoothed = [s + d for s, d in zip(smoothed, direct)]
         arrive(t, even)
         residual = far_part(t, even, residual)
+
         for j in range(comp):
             part[pair, pl.ds(j, tiles, stride=comp), :] = residual[j]
         give_part(pair).start()
+        give_more(pair == 0, 0, 1)
+        give_more(again, 6)
         arrive(t, across)
         residual = far_part(t, across, residual)
         advance(t, direct, residual)
         send(t + 1, field.at[t + 1], across).start()
+        if closing:
+            @pl.when(feeds & again)
+            def _():
+                feed(t + 1).start()
+        give_more(pair == 0, 2)
 
         direct, residual = own_part(t + 1, residual)
         smoothed = [s + d for s, d in zip(smoothed, direct)]
 
         @pl.when(pair == 0)
         def _():
-            for i in range(3):
-                give(i).wait_recv()
+            for copy in give():
+                copy.wait_recv()
+
         give_part(pair).wait_recv()
         other = [ghost_part[pair, pl.ds(j, tiles, stride=comp), :] for j in range(comp)]
-        other = combine(0, taken(field.at[t], ghost_lane[...], ghost_tile[...]), other, ghost_values)
-        for j in range(comp):
-            beside[t + 1, across, pl.ds(j, tiles, stride=comp), :] = (
-                coef[t, 0] * beside[t, across, pl.ds(j, tiles, stride=comp), :] + coef[t, 1] * other[j]
-            )
+        k = 2 - across
+        foresee(t, combine(k, taken(field.at[t], ghost_local[k]), other, ghost_values))
+        give_more(pair == 0, 3)
         residual = far_part(t + 1, across, residual)
         arrive(t + 1, even)
         residual = far_part(t + 1, even, residual)
         advance(t + 1, direct, residual)
-        for way in (even, across):
-            send(t + 2, field.at[t + 2], way).start()
+        send(t + 2, field.at[t + 2], across).start()
+
+        @pl.when(jnp.logical_not(first & again) if closing else True)
+        def _():
+            send(t + 2, field.at[t + 2], even).start()
+        give_more(pair == 0, 4, 5)
         return smoothed, residual
 
     smoothed = [jnp.zeros((tiles, LANES), jnp.float32) for j in range(comp)]
@@ -241,9 +311,20 @@
     direct, residual = own_part(STEPS, residual)
     for j in range(comp):
         smoothed_out[pl.ds(j, tiles, stride=comp), :] = smoothed[j] + direct[j]
-    for way in (even, across):
-        arrive(STEPS, way)
-        residual = far_part(STEPS, way, residual)
+    arrive(STEPS, even)
+    residual = far_part(STEPS, even, residual)
+
+    @pl.when(jnp.logical_not(last) if closing else True)
+    def _():
+        arrive(STEPS, across)
+    if closing:
+        @pl.when(last)
+        def _():
+            for i in range(pieces):
+                for copy in give_rest(i):
+                    copy.wait_recv()
+            foresee_alone(STEPS - 1)
+    residual = far_part(STEPS, across, residual)
 
     squares = residual[0] * residual[0]
     for j in range(1, comp):
@@ -264,11 +345,23 @@
         for t in range(STEPS + 1):
             send(t, field.at[t], across).wait_send()
             if t % 2 == 0:
-                send(t, field.at[t], even).wait_send()
+                @pl.when(jnp.logical_not(first) if closing and t == STEPS else True)
+                def _():
+                    send(t, field.at[t], even).wait_send()
         for pair in range(STEPS // 2):
             give_part(pair).wait_send()
-        for i in range(3):
-            give(i).wait_send()
+        for copy in give():
+            copy.wait_send()
+        if closing:
+            @pl.when(first)
+            def _():
+                for i in range(pieces):
+                    for copy in give_rest(i):
+                        copy.wait_send()
+
+            @pl.when(feeds)
+            def _():
+                feed(STEPS - 1).wait_send()
 
     near_sums[near_me] = partial
     for partner in near_partners:
@@ -345,13 +438,13 @@
             pltpu.VMEM((STEPS + 1,) + plane, f32),
             pltpu.VMEM((STEPS + 1, 2) + plane, f32),
             pltpu.VMEM((blocks, tiles, LANES), jnp.int32),
-            pltpu.VMEM((blocks, tiles, LANES), jnp.int32),
             pltpu.VMEM((STEPS, 2, tiles, LANES), f32),
             pltpu.VMEM((near, 1, LANES), f32),
             pltpu.VMEM((far, 1, LANES), f32),
-            pltpu.VMEM((comp * comp * tiles, LANES), f32),
-            pltpu.VMEM((tiles, LANES), jnp.int32),
-            pltpu.VMEM((tiles, LANES), jnp.int32),
+            pltpu.VMEM((blocks * comp * comp * tiles, LANES), f32),
+            pltpu.VMEM((blocks, tiles, LANES), jnp.int32),
+            pltpu.VMEM(plane, f32),
+            pltpu.VMEM((STEPS + 1,) + plane, f32),
             pltpu.VMEM((STEPS // 2,) + plane, f32),
             pltpu.VMEM((STEPS // 2,) + plane, f32),
             dma((blocks,)),
@@ -360,10 +453,12 @@
             dma((STEPS + 1, 2)),
             dma((2,)),
             dma((2,)),
-            dma((3,)),
-            dma((3,)),
+            dma((blocks + 3,)),
+            dma((blocks + 3,)),
             dma((STEPS // 2,)),
             dma((STEPS // 2,)),
+            dma((STEPS + 1,)),
+            dma((STEPS + 1,)),
         ],
         compiler_params=pltpu.CompilerParams(collective_id=0, has_side_effects=True, vmem_limit_bytes=8 * 1024 * 1024),
     )(

time: 29.1 us -> 26.4 us (0.907)
  Pallas kernels: 27 us -> 24.3 us
    pallas_call x1, Pallas kernels: 26.4 us -> 23.7 us  [shards(): pl.pallas_call(functools.partial(kernel, subs, aggs, (blocks, comp, tiles...]
where the time goes in v5:
time: 26.4 us; the launch traced here: 26.2 us
  Pallas kernels  24.3 us (92%)
  between operations  1.93 us (7%)
    pallas_call x1, Pallas kernels, shards(): pl.pallas_call(functools.partial(kernel, subs, aggs, (blocks, comp, tiles...  23.7 us
    pallas_call x1, Pallas kernels, shards(): pl.pallas_call(put_out, out_shape=(jax.ShapeDtypeStruct(plane, f32), jax....  0.64 us

profile of v5, /device:TPU:0, one launch (start us, length us, event | category | flops | bytes accessed | tf_op | source)
XLA Modules:
  0.0 26.2 jit_solution(11802924335576424927)
XLA Ops:
  1.9 23.7 %shard_map.85 = (f32[32,128]{1,0:T(8,128)S(1)}, f32[32,128]{1,0:T(8,128)S(1)}, f32[8,128]{1,0:T(8,128)S(1)}) custom-call(f32[896,128]{1,0:T(8,128)} %bitcast.27, s32[7,1024]{1,0:T(8,128)} %cols_hbm.1, f32[32,128]{1,0:T(8,128)} %bitcast.28, f32[32,128]{1,0:T(8,128)} %bitcast.29, s32[1]{0:T(128)S(6)} %copy.14.low_ref, s32[1]{0:T(128)S(6)} %copy.15.high_ref), custom_call_target="tpu_custom_call" | custom-call | tf_op jit(solution)/shard_map/pallas_call | solution.py:424
  25.6 0.6 %shard_map.86 = (f32[32,128]{1,0:T(8,128)}, f32[32,128]{1,0:T(8,128)}, f32[1,128]{1,0:T(1,128)}) custom-call(f32[32,128]{1,0:T(8,128)S(1)} %get-tuple-element.9.refs_0_, f32[32,128]{1,0:T(8,128)S(1)} %get-tuple-element.10.refs_1_, f32[8,128]{1,0:T(8,128)S(1)} %get-tuple-element.11.refs_2_), custom_call_target="tpu_custom_call" | custom-call | tf_op jit(solution)/shard_map/pallas_call | solution.py:473

commit v6 on v5

--- a/solution.py
+++ b/solution.py
@@ -24,28 +24,18 @@
     values, cols, cols_flat, rhs, field, beside, local_of, coef,
     near_sums, far_sums,
     ghost_values, ghost_local, ghost_residual, beyond, part, ghost_part,
-    values_sem, load_sem, send_sem, recv_sem,
-    near_sems, far_sems,
-    ghost_send, ghost_recv, part_send, part_recv, beyond_send, beyond_recv,
+    load_sem, chip_sem, cross_sem, ghost_sem, sum_sem,
 ):
     blocks, comp, tiles = shape
     devices = subs * aggs
     rows = tiles * LANES
     load_cols = pltpu.make_async_copy(cols_hbm, cols, load_sem.at[0])
     load_guess = pltpu.make_async_copy(guess_hbm, field.at[0], load_sem.at[1])
-    load_rhs = pltpu.make_async_copy(rhs_hbm, rhs, load_sem.at[2])
-    for load in (load_guess, load_cols):
-        load.start()
+    load_rhs = pltpu.make_async_copy(rhs_hbm, rhs, load_sem.at[3])
+    load_values = pltpu.make_async_copy(values_hbm, values, load_sem.at[2])
     own = [0] + list(range(3, blocks))
     per_block = comp * comp * tiles
 
-    def load_values(k):
-        part = pl.ds(k * per_block, per_block)
-        return pltpu.make_async_copy(values_hbm.at[part], values.at[part], values_sem.at[k])
-
-    for k in own + [1, 2]:
-        load_values(k).start()
-    load_rhs.start()
 
     sub, agg = lax.axis_index("sub"), lax.axis_index("agg")
     me = sub * aggs + agg
@@ -67,8 +57,10 @@
     previous = ahead_of(me, devices - 1, devices)
     one_round = devices <= ONE_ROUND
     if one_round:
-        near_steps = [(a, b) for a in range(subs) for b in range(aggs)][1:]
-        near_steps.sort(key=lambda step: min(step[0], subs - step[0]))
+        low = sub < subs // 2
+        near_steps = [
+            (jnp.where(low, subs - a, a), b) for a in range(1, subs) for b in range(aggs)
+        ] + [(0, b) for b in range(1, aggs)]
         near, near_me = devices, me
         far_steps = []
     else:
@@ -81,7 +73,9 @@
     even = 1 - lax.rem(me, 2)
     across = 1 - even
     closing = one_round and devices >= 4
-    first, last, feeds = me == 0, me == devices - 1, me == 1
+    first, last = me == 0, me == devices - 1
+    gives = takes = first | last
+    feeds = (me == 1) | (me == devices - 2)
 
     barrier = pltpu.get_barrier_semaphore()
     partners = far_partners + near_partners
@@ -89,6 +83,8 @@
         partners = [ring(0), ring(1)] + partners
     for partner in partners:
         pl.semaphore_signal(barrier, inc=1, device_id=partner, device_id_type=MESH)
+    for load in (load_guess, load_cols, load_values, load_rhs):
+        load.start()
 
     load_guess.wait()
     pl.semaphore_wait(barrier, len(partners))
@@ -97,21 +93,23 @@
         return pltpu.make_async_remote_copy(
             src_ref=source,
             dst_ref=beside.at[step, way],
-            send_sem=send_sem.at[step, way],
-            recv_sem=recv_sem.at[step, way],
+            send_sem=cross_sem.at[0] if way is even else chip_sem.at[0],
+            recv_sem=(
+                cross_sem.at[1 + lax.div(step, 2)] if way is even else chip_sem.at[1 + lax.rem(step, 2)]
+            ),
             device_id=ring(way),
             device_id_type=MESH,
         )
 
-    for way in range(2):
+    for way in (even, across):
         send(0, field.at[0], way).start()
 
     def over(source, target, i):
         return pltpu.make_async_remote_copy(
             src_ref=source,
             dst_ref=target,
-            send_sem=ghost_send.at[i],
-            recv_sem=ghost_recv.at[i],
+            send_sem=ghost_sem.at[2 * i],
+            recv_sem=ghost_sem.at[2 * i + 1],
             device_id=ring(even),
             device_id_type=MESH,
         )
@@ -121,7 +119,7 @@
         piece = pl.ds(k * per_block, per_block)
         return [
             over(values.at[piece], ghost_values.at[piece], 0),
-            over(local_of.at[k], ghost_local.at[k], 1),
+            over(local_of.at[k], ghost_local.at[k], 0),
         ]
 
     def give_rest(i):
@@ -129,30 +127,38 @@
         if i == 0:
             tail = pl.ds(3, blocks - 3)
             return [
-                over(local_of.at[tail], ghost_local.at[tail], 2),
-                over(local_of.at[k], ghost_local.at[k], 3),
+                over(local_of.at[tail], ghost_local.at[tail], 1),
+                over(local_of.at[k], ghost_local.at[k], 1),
             ]
         block = k if i == 2 else own[max(i - 2, 0)]
         piece = pl.ds(block * per_block, per_block)
-        return [over(values.at[piece], ghost_values.at[piece], 3 + i)]
-
-    pieces = blocks
+        return [over(values.at[piece], ghost_values.at[piece], 1)]
+
+    def given(count, i):
+        some = pl.ds(0, count)
+        return over(values.at[some], ghost_values.at[some], i)
+
+    block_given = given(per_block + tiles, 0)
+    rest_given = given((blocks - 1) * per_block + (blocks - 2) * tiles, 1)
 
     def give_more(*which):
         if closing and which:
-            @pl.when(first & which[0])
-            def _():
-                for i in which[1:]:
-                    for copy in give_rest(i):
-                        copy.start()
+            for giver, some in ((first, which[1]), (last, which[2])):
+                if some:
+                    @pl.when(giver & which[0])
+                    def _():
+                        for i in some:
+                            for copy in give_rest(i):
+                                copy.start()
 
     def feed(t):
+        to = jnp.where(me == 1, devices - 1, 0)
         return pltpu.make_async_remote_copy(
             src_ref=field.at[t],
             dst_ref=beyond.at[t],
-            send_sem=beyond_send.at[t],
-            recv_sem=beyond_recv.at[t],
-            device_id=((devices - 1) // aggs, (devices - 1) % aggs),
+            send_sem=ghost_sem.at[4],
+            recv_sem=ghost_sem.at[5],
+            device_id=(to // aggs, lax.rem(to, aggs)),
             device_id_type=MESH,
         )
 
@@ -160,8 +166,8 @@
         return pltpu.make_async_remote_copy(
             src_ref=part.at[t],
             dst_ref=ghost_part.at[t],
-            send_sem=part_send.at[t],
-            recv_sem=part_recv.at[t],
+            send_sem=cross_sem.at[0],
+            recv_sem=cross_sem.at[2 + STEPS // 2 + t],
             device_id=ring(even),
             device_id_type=MESH,
         )
@@ -219,7 +225,7 @@
         return combine(k, taken(beside.at[t, way], local_of[k]), residual)
 
     def arrive(t, way):
-        send(t, field.at[t], way).wait_recv()
+        send(t, field.at[t], across if way is even else even).wait_recv()
 
     def advance(t, direct, residual):
         for j in range(comp):
@@ -228,8 +234,7 @@
             )
 
     load_rhs.wait()
-    for k in own + [1, 2]:
-        load_values(k).wait()
+    load_values.wait()
     for copy in give():
         copy.start()
 
@@ -267,8 +272,8 @@
         for j in range(comp):
             part[pair, pl.ds(j, tiles, stride=comp), :] = residual[j]
         give_part(pair).start()
-        give_more(pair == 0, 0, 1)
-        give_more(again, 6)
+        give_more(pair == 0, (0, 1), (0, 1))
+        give_more(again, (5, 6), (5, 6))
         arrive(t, across)
         residual = far_part(t, across, residual)
         advance(t, direct, residual)
@@ -277,31 +282,30 @@
             @pl.when(feeds & again)
             def _():
                 feed(t + 1).start()
-        give_more(pair == 0, 2)
+        give_more(pair == 0, (2,), (2,))
 
         direct, residual = own_part(t + 1, residual)
         smoothed = [s + d for s, d in zip(smoothed, direct)]
 
         @pl.when(pair == 0)
         def _():
-            for copy in give():
-                copy.wait_recv()
+            block_given.wait_recv()
 
         give_part(pair).wait_recv()
         other = [ghost_part[pair, pl.ds(j, tiles, stride=comp), :] for j in range(comp)]
         k = 2 - across
         foresee(t, combine(k, taken(field.at[t], ghost_local[k]), other, ghost_values))
-        give_more(pair == 0, 3)
+        give_more(pair == 0, (), ())
         residual = far_part(t + 1, across, residual)
         arrive(t + 1, even)
         residual = far_part(t + 1, even, residual)
         advance(t + 1, direct, residual)
         send(t + 2, field.at[t + 2], across).start()
 
-        @pl.when(jnp.logical_not(first & again) if closing else True)
+        @pl.when(jnp.logical_not(gives & again) if closing else True)
         def _():
             send(t + 2, field.at[t + 2], even).start()
-        give_more(pair == 0, 4, 5)
+        give_more(pair == 0, (3, 4), (3, 4))
         return smoothed, residual
 
     smoothed = [jnp.zeros((tiles, LANES), jnp.float32) for j in range(comp)]
@@ -314,15 +318,13 @@
     arrive(STEPS, even)
     residual = far_part(STEPS, even, residual)
 
-    @pl.when(jnp.logical_not(last) if closing else True)
+    @pl.when(jnp.logical_not(takes) if closing else True)
     def _():
         arrive(STEPS, across)
     if closing:
-        @pl.when(last)
+        @pl.when(takes)
         def _():
-            for i in range(pieces):
-                for copy in give_rest(i):
-                    copy.wait_recv()
+            rest_given.wait_recv()
             foresee_alone(STEPS - 1)
     residual = far_part(STEPS, across, residual)
 
@@ -341,23 +343,29 @@
             device_id_type=MESH,
         )
 
+    def sent(count, way):
+        planes = pl.ds(0, count)
+        return pltpu.make_async_remote_copy(
+            src_ref=field.at[planes],
+            dst_ref=beyond.at[planes],
+            send_sem=cross_sem.at[0] if way is even else chip_sem.at[0],
+            recv_sem=ghost_sem.at[5],
+            device_id=ring(way),
+            device_id_type=MESH,
+        )
+
     def wait_sends():
-        for t in range(STEPS + 1):
-            send(t, field.at[t], across).wait_send()
-            if t % 2 == 0:
-                @pl.when(jnp.logical_not(first) if closing and t == STEPS else True)
-                def _():
-                    send(t, field.at[t], even).wait_send()
-        for pair in range(STEPS // 2):
-            give_part(pair).wait_send()
-        for copy in give():
-            copy.wait_send()
+        sent(STEPS + 1, across).wait_send()
+        block_given.wait_send()
+
+        @pl.when(jnp.logical_not(gives) if closing else True)
+        def _():
+            sent(STEPS + 1, even).wait_send()
         if closing:
-            @pl.when(first)
+            @pl.when(gives)
             def _():
-                for i in range(pieces):
-                    for copy in give_rest(i):
-                        copy.wait_send()
+                sent(STEPS, even).wait_send()
+                rest_given.wait_send()
 
             @pl.when(feeds)
             def _():
@@ -365,25 +373,26 @@
 
     near_sums[near_me] = partial
     for partner in near_partners:
-        spread_sums(near_sums, near_me, partner, near_sems).start()
+        spread_sums(near_sums, near_me, partner, sum_sem.at[pl.ds(0, 2)]).start()
     for j in range(comp):
         residual_out[pl.ds(j, tiles, stride=comp), :] = residual[j]
     wait_sends()
     if near_partners:
-        every = pl.ds(0, len(near_partners))
-        spread_sums(near_sums, every, near_partners[0], near_sems).wait_send()
-        spread_sums(near_sums, every, near_partners[0], near_sems).wait_recv()
+        every_near = pl.ds(0, len(near_partners))
+        spread_sums(near_sums, every_near, near_partners[0], sum_sem.at[pl.ds(0, 2)]).wait_recv()
     total = jnp.sum(near_sums[...], axis=0)
     if far_partners:
         far_sums[sub] = total
         for partner in far_partners:
-            spread_sums(far_sums, sub, partner, far_sems).start()
+            spread_sums(far_sums, sub, partner, sum_sem.at[pl.ds(2, 2)]).start()
         every = pl.ds(0, len(far_partners))
-        spread_sums(far_sums, every, far_partners[0], far_sems).wait_send()
-        spread_sums(far_sums, every, far_partners[0], far_sems).wait_recv()
+        spread_sums(far_sums, every, far_partners[0], sum_sem.at[pl.ds(2, 2)]).wait_send()
+        spread_sums(far_sums, every, far_partners[0], sum_sem.at[pl.ds(2, 2)]).wait_recv()
         total = jnp.sum(far_sums[...], axis=0)
     count = float(comp * rows * devices)
     rms_ref[...] = jnp.broadcast_to(jnp.sqrt(jnp.sum(total, axis=1, keepdims=True) / count + 1e-06), rms_ref.shape)
+    if near_partners:
+        spread_sums(near_sums, every_near, near_partners[0], sum_sem.at[pl.ds(0, 2)]).wait_send()
 
 
 def put_out(*refs):
@@ -447,18 +456,11 @@
             pltpu.VMEM((STEPS + 1,) + plane, f32),
             pltpu.VMEM((STEPS // 2,) + plane, f32),
             pltpu.VMEM((STEPS // 2,) + plane, f32),
-            dma((blocks,)),
-            dma((5,)),
-            dma((STEPS + 1, 2)),
-            dma((STEPS + 1, 2)),
-            dma((2,)),
-            dma((2,)),
-            dma((blocks + 3,)),
-            dma((blocks + 3,)),
-            dma((STEPS // 2,)),
-            dma((STEPS // 2,)),
-            dma((STEPS + 1,)),
-            dma((STEPS + 1,)),
+            dma((4,)),
+            dma((3,)),
+            dma((2 + STEPS,)),
+            dma((6,)),
+            dma((2 if far == 1 else 4,)),
         ],
         compiler_params=pltpu.CompilerParams(collective_id=0, has_side_effects=True, vmem_limit_bytes=8 * 1024 * 1024),
     )(

time: 26.4 us -> 26 us (0.985)
  Pallas kernels: 24.3 us -> 23.8 us
    pallas_call x1, Pallas kernels: 23.7 us -> 23.2 us  [shards(): pl.pallas_call(functools.partial(kernel, subs, aggs, (blocks, comp, tiles...]
where the time goes in v6:
time: 26 us; the launch traced here: 25.8 us
  Pallas kernels  23.8 us (92%)
  between operations  1.93 us (7%)
    pallas_call x1, Pallas kernels, shards(): pl.pallas_call(functools.partial(kernel, subs, aggs, (blocks, comp, tiles...  23.2 us
    pallas_call x1, Pallas kernels, shards(): pl.pallas_call(put_out, out_shape=(jax.ShapeDtypeStruct(plane, f32), jax....  0.64 us

profile of v6, /device:TPU:0, one launch (start us, length us, event | category | flops | bytes accessed | tf_op | source)
XLA Modules:
  0.0 25.8 jit_solution(14411690469032884575)
XLA Ops:
  1.9 23.2 %shard_map.85 = (f32[32,128]{1,0:T(8,128)S(1)}, f32[32,128]{1,0:T(8,128)S(1)}, f32[8,128]{1,0:T(8,128)S(1)}) custom-call(f32[896,128]{1,0:T(8,128)} %bitcast.27, s32[7,1024]{1,0:T(8,128)} %cols_hbm.1, f32[32,128]{1,0:T(8,128)} %bitcast.28, f32[32,128]{1,0:T(8,128)} %bitcast.29, s32[1]{0:T(128)S(6)} %copy.14.low_ref, s32[1]{0:T(128)S(6)} %copy.15.high_ref), custom_call_target="tpu_custom_call" | custom-call | tf_op jit(solution)/shard_map/pallas_call | solution.py:433
  25.1 0.6 %shard_map.86 = (f32[32,128]{1,0:T(8,128)}, f32[32,128]{1,0:T(8,128)}, f32[1,128]{1,0:T(1,128)}) custom-call(f32[32,128]{1,0:T(8,128)S(1)} %get-tuple-element.9.refs_0_, f32[32,128]{1,0:T(8,128)S(1)} %get-tuple-element.10.refs_1_, f32[8,128]{1,0:T(8,128)S(1)} %get-tuple-element.11.refs_2_), custom_call_target="tpu_custom_call" | custom-call | tf_op jit(solution)/shard_map/pallas_call | solution.py:475

commit v7 on v6

--- a/solution.py
+++ b/solution.py
@@ -74,8 +74,7 @@
     across = 1 - even
     closing = one_round and devices >= 4
     first, last = me == 0, me == devices - 1
-    gives = takes = first | last
-    feeds = (me == 1) | (me == devices - 2)
+    gives, takes, feeds = first, last, me == 1
 
     barrier = pltpu.get_barrier_semaphore()
     partners = far_partners + near_partners
@@ -86,8 +85,6 @@
     for load in (load_guess, load_cols, load_values, load_rhs):
         load.start()
 
-    load_guess.wait()
-    pl.semaphore_wait(barrier, len(partners))
 
     def send(step, source, way):
         return pltpu.make_async_remote_copy(
@@ -95,14 +92,12 @@
             dst_ref=beside.at[step, way],
             send_sem=cross_sem.at[0] if way is even else chip_sem.at[0],
             recv_sem=(
-                cross_sem.at[1 + lax.div(step, 2)] if way is even else chip_sem.at[1 + lax.rem(step, 2)]
+                cross_sem.at[1] if way is even else chip_sem.at[1 + lax.rem(step, 2)]
             ),
             device_id=ring(way),
             device_id_type=MESH,
         )
 
-    for way in (even, across):
-        send(0, field.at[0], way).start()
 
     def over(source, target, i):
         return pltpu.make_async_remote_copy(
@@ -141,15 +136,13 @@
     block_given = given(per_block + tiles, 0)
     rest_given = given((blocks - 1) * per_block + (blocks - 2) * tiles, 1)
 
-    def give_more(*which):
+    def give_more(when, *which):
         if closing and which:
-            for giver, some in ((first, which[1]), (last, which[2])):
-                if some:
-                    @pl.when(giver & which[0])
-                    def _():
-                        for i in some:
-                            for copy in give_rest(i):
-                                copy.start()
+            @pl.when(first & when)
+            def _():
+                for i in which:
+                    for copy in give_rest(i):
+                        copy.start()
 
     def feed(t):
         to = jnp.where(me == 1, devices - 1, 0)
@@ -167,7 +160,7 @@
             src_ref=part.at[t],
             dst_ref=ghost_part.at[t],
             send_sem=cross_sem.at[0],
-            recv_sem=cross_sem.at[2 + STEPS // 2 + t],
+            recv_sem=cross_sem.at[2 + t],
             device_id=ring(even),
             device_id_type=MESH,
         )
@@ -233,10 +226,14 @@
                 coef[t, 0] * direct[j] + coef[t, 1] * residual[j]
             )
 
-    load_rhs.wait()
+    load_guess.wait()
+    pl.semaphore_wait(barrier, len(partners))
+    for way in (even, across):
+        send(0, field.at[0], way).start()
     load_values.wait()
     for copy in give():
         copy.start()
+    load_rhs.wait()
 
     def foresee(t, total):
         source = beside.at[t, across]
@@ -260,57 +257,52 @@
         total = combine(k, taken(beyond.at[t], ghost_local[k]), total, ghost_values)
         foresee(t, total)
 
-    def two_steps(pair, carry):
+    def foresee_from(t):
+        give_part(t).wait_recv()
+        other = [ghost_part[t, pl.ds(j, tiles, stride=comp), :] for j in range(comp)]
+        k = 2 - across
+        foresee(t, combine(k, taken(field.at[t], ghost_local[k]), other, ghost_values))
+
+    def step(t, carry):
         smoothed, residual = carry
-        t = 2 * pair
-        again = pair > 0
         direct, residual = own_part(t, residual)
         smoothed = [s + d for s, d in zip(smoothed, direct)]
         arrive(t, even)
         residual = far_part(t, even, residual)
 
-        for j in range(comp):
-            part[pair, pl.ds(j, tiles, stride=comp), :] = residual[j]
-        give_part(pair).start()
-        give_more(pair == 0, (0, 1), (0, 1))
-        give_more(again, (5, 6), (5, 6))
-        arrive(t, across)
+        @pl.when(jnp.logical_not(first & (t == STEPS - 1)) if closing else True)
+        def _():
+            for j in range(comp):
+                part[t, pl.ds(j, tiles, stride=comp), :] = residual[j]
+            give_part(t).start()
+        give_more(t == 0, 0, 1)
+        give_more(t == 2, 5, 6)
+
+        @pl.when(t == 0)
+        def _():
+            arrive(0, across)
+
+        @pl.when(t == 1)
+        def _():
+            block_given.wait_recv()
+
+        @pl.when(t > 0)
+        def _():
+            foresee_from(t - 1)
         residual = far_part(t, across, residual)
         advance(t, direct, residual)
         send(t + 1, field.at[t + 1], across).start()
         if closing:
-            @pl.when(feeds & again)
+            @pl.when(feeds & (t == STEPS - 2))
             def _():
                 feed(t + 1).start()
-        give_more(pair == 0, (2,), (2,))
-
-        direct, residual = own_part(t + 1, residual)
-        smoothed = [s + d for s, d in zip(smoothed, direct)]
-
-        @pl.when(pair == 0)
-        def _():
-            block_given.wait_recv()
-
-        give_part(pair).wait_recv()
-        other = [ghost_part[pair, pl.ds(j, tiles, stride=comp), :] for j in range(comp)]
-        k = 2 - across
-        foresee(t, combine(k, taken(field.at[t], ghost_local[k]), other, ghost_values))
-        give_more(pair == 0, (), ())
-        residual = far_part(t + 1, across, residual)
-        arrive(t + 1, even)
-        residual = far_part(t + 1, even, residual)
-        advance(t + 1, direct, residual)
-        send(t + 2, field.at[t + 2], across).start()
-
-        @pl.when(jnp.logical_not(gives & again) if closing else True)
-        def _():
-            send(t + 2, field.at[t + 2], even).start()
-        give_more(pair == 0, (3, 4), (3, 4))
+        give_more(t == 0, 2)
+        give_more(t == 1, 3, 4)
         return smoothed, residual
 
     smoothed = [jnp.zeros((tiles, LANES), jnp.float32) for j in range(comp)]
     residual = [rhs[pl.ds(j, tiles, stride=comp), :] for j in range(comp)]
-    smoothed, residual = lax.fori_loop(0, STEPS // 2, two_steps, (smoothed, residual))
+    smoothed, residual = lax.fori_loop(0, STEPS, step, (smoothed, residual))
 
     direct, residual = own_part(STEPS, residual)
     for j in range(comp):
@@ -320,7 +312,7 @@
 
     @pl.when(jnp.logical_not(takes) if closing else True)
     def _():
-        arrive(STEPS, across)
+        foresee_from(STEPS - 1)
     if closing:
         @pl.when(takes)
         def _():
@@ -454,8 +446,8 @@
             pltpu.VMEM((blocks, tiles, LANES), jnp.int32),
             pltpu.VMEM(plane, f32),
             pltpu.VMEM((STEPS + 1,) + plane, f32),
-            pltpu.VMEM((STEPS // 2,) + plane, f32),
-            pltpu.VMEM((STEPS // 2,) + plane, f32),
+            pltpu.VMEM((STEPS,) + plane, f32),
+            pltpu.VMEM((STEPS,) + plane, f32),
             dma((4,)),
             dma((3,)),
             dma((2 + STEPS,)),

time: 26 us -> 25.4 us (0.977)
  Pallas kernels: 23.8 us -> 23.2 us
    pallas_call x1, Pallas kernels: 23.2 us -> 22.6 us  [shards(): pl.pallas_call(functools.partial(kernel, subs, aggs, (blocks, comp, tiles...]
where the time goes in v7:
time: 25.4 us; the launch traced here: 25.2 us
  Pallas kernels  23.2 us (91%)
  between operations  1.93 us (8%)
    pallas_call x1, Pallas kernels, shards(): pl.pallas_call(functools.partial(kernel, subs, aggs, (blocks, comp, tiles...  22.6 us
    pallas_call x1, Pallas kernels, shards(): pl.pallas_call(put_out, out_shape=(jax.ShapeDtypeStruct(plane, f32), jax....  0.64 us

profile of v7, /device:TPU:0, one launch (start us, length us, event | category | flops | bytes accessed | tf_op | source)
XLA Modules:
  0.0 25.2 jit_solution(10104340680579187283)
XLA Ops:
  1.9 22.6 %shard_map.85 = (f32[32,128]{1,0:T(8,128)S(1)}, f32[32,128]{1,0:T(8,128)S(1)}, f32[8,128]{1,0:T(8,128)S(1)}) custom-call(f32[896,128]{1,0:T(8,128)} %bitcast.27, s32[7,1024]{1,0:T(8,128)} %cols_hbm.1, f32[32,128]{1,0:T(8,128)} %bitcast.28, f32[32,128]{1,0:T(8,128)} %bitcast.29, s32[1]{0:T(128)S(6)} %copy.14.low_ref, s32[1]{0:T(128)S(6)} %copy.15.high_ref), custom_call_target="tpu_custom_call" | custom-call | tf_op jit(solution)/shard_map/pallas_call | solution.py:425
  24.5 0.6 %shard_map.86 = (f32[32,128]{1,0:T(8,128)}, f32[32,128]{1,0:T(8,128)}, f32[1,128]{1,0:T(1,128)}) custom-call(f32[32,128]{1,0:T(8,128)S(1)} %get-tuple-element.9.refs_0_, f32[32,128]{1,0:T(8,128)S(1)} %get-tuple-element.10.refs_1_, f32[8,128]{1,0:T(8,128)S(1)} %get-tuple-element.11.refs_2_), custom_call_target="tpu_custom_call" | custom-call | tf_op jit(solution)/shard_map/pallas_call | solution.py:467

commit v8 on v7

--- a/solution.py
+++ b/solution.py
@@ -258,10 +258,11 @@
         foresee(t, total)
 
     def foresee_from(t):
+        k = 2 - across
+        mine = [jnp.zeros((tiles, LANES), jnp.float32) for j in range(comp)]
+        mine = combine(k, taken(field.at[t], ghost_local[k]), mine, ghost_values)
         give_part(t).wait_recv()
-        other = [ghost_part[t, pl.ds(j, tiles, stride=comp), :] for j in range(comp)]
-        k = 2 - across
-        foresee(t, combine(k, taken(field.at[t], ghost_local[k]), other, ghost_values))
+        foresee(t, [ghost_part[t, pl.ds(j, tiles, stride=comp), :] + mine[j] for j in range(comp)])
 
     def step(t, carry):
         smoothed, residual = carry

time: 25.4 us -> 25.4 us (level)
  no operation moved by 1% of the time
where the time goes in v8:
time: 25.4 us; the launch traced here: 25.2 us
  Pallas kernels  23.2 us (91%)
  between operations  1.93 us (8%)
    pallas_call x1, Pallas kernels, shards(): pl.pallas_call(functools.partial(kernel, subs, aggs, (blocks, comp, tiles...  22.6 us
    pallas_call x1, Pallas kernels, shards(): pl.pallas_call(put_out, out_shape=(jax.ShapeDtypeStruct(plane, f32), jax....  0.64 us

profile of v8, /device:TPU:0, one launch (start us, length us, event | category | flops | bytes accessed | tf_op | source)
XLA Modules:
  0.0 25.2 jit_solution(2078750063443640167)
XLA Ops:
  1.9 22.6 %shard_map.85 = (f32[32,128]{1,0:T(8,128)S(1)}, f32[32,128]{1,0:T(8,128)S(1)}, f32[8,128]{1,0:T(8,128)S(1)}) custom-call(f32[896,128]{1,0:T(8,128)} %bitcast.27, s32[7,1024]{1,0:T(8,128)} %cols_hbm.1, f32[32,128]{1,0:T(8,128)} %bitcast.28, f32[32,128]{1,0:T(8,128)} %bitcast.29, s32[1]{0:T(128)S(6)} %copy.14.low_ref, s32[1]{0:T(128)S(6)} %copy.15.high_ref), custom_call_target="tpu_custom_call" | custom-call | tf_op jit(solution)/shard_map/pallas_call | solution.py:426
  24.5 0.6 %shard_map.86 = (f32[32,128]{1,0:T(8,128)}, f32[32,128]{1,0:T(8,128)}, f32[1,128]{1,0:T(1,128)}) custom-call(f32[32,128]{1,0:T(8,128)S(1)} %get-tuple-element.9.refs_0_, f32[32,128]{1,0:T(8,128)S(1)} %get-tuple-element.10.refs_1_, f32[8,128]{1,0:T(8,128)S(1)} %get-tuple-element.11.refs_2_), custom_call_target="tpu_custom_call" | custom-call | tf_op jit(solution)/shard_map/pallas_call | solution.py:468

commit v9 on v8

--- a/solution.py
+++ b/solution.py
@@ -303,7 +303,7 @@
 
     smoothed = [jnp.zeros((tiles, LANES), jnp.float32) for j in range(comp)]
     residual = [rhs[pl.ds(j, tiles, stride=comp), :] for j in range(comp)]
-    smoothed, residual = lax.fori_loop(0, STEPS, step, (smoothed, residual))
+    smoothed, residual = lax.fori_loop(0, STEPS, step, (smoothed, residual), unroll=True)
 
     direct, residual = own_part(STEPS, residual)
     for j in range(comp):

time: 25.4 us -> 25.4 us (level)
  no operation moved by 1% of the time
where the time goes in v9:
time: 25.4 us; the launch traced here: 25.2 us
  Pallas kernels  23.2 us (91%)
  between operations  1.93 us (8%)
    pallas_call x1, Pallas kernels, shards(): pl.pallas_call(functools.partial(kernel, subs, aggs, (blocks, comp, tiles...  22.6 us
    pallas_call x1, Pallas kernels, shards(): pl.pallas_call(put_out, out_shape=(jax.ShapeDtypeStruct(plane, f32), jax....  0.64 us

profile of v9, /device:TPU:0, one launch (start us, length us, event | category | flops | bytes accessed | tf_op | source)
XLA Modules:
  0.0 25.2 jit_solution(6300617900296596415)
XLA Ops:
  1.9 22.6 %shard_map.85 = (f32[32,128]{1,0:T(8,128)S(1)}, f32[32,128]{1,0:T(8,128)S(1)}, f32[8,128]{1,0:T(8,128)S(1)}) custom-call(f32[896,128]{1,0:T(8,128)} %bitcast.27, s32[7,1024]{1,0:T(8,128)} %cols_hbm.1, f32[32,128]{1,0:T(8,128)} %bitcast.28, f32[32,128]{1,0:T(8,128)} %bitcast.29, s32[1]{0:T(128)S(6)} %copy.14.low_ref, s32[1]{0:T(128)S(6)} %copy.15.high_ref), custom_call_target="tpu_custom_call" | custom-call | tf_op jit(solution)/shard_map/pallas_call | solution.py:426
  24.5 0.6 %shard_map.86 = (f32[32,128]{1,0:T(8,128)}, f32[32,128]{1,0:T(8,128)}, f32[1,128]{1,0:T(1,128)}) custom-call(f32[32,128]{1,0:T(8,128)S(1)} %get-tuple-element.9.refs_0_, f32[32,128]{1,0:T(8,128)S(1)} %get-tuple-element.10.refs_1_, f32[8,128]{1,0:T(8,128)S(1)} %get-tuple-element.11.refs_2_), custom_call_target="tpu_custom_call" | custom-call | tf_op jit(solution)/shard_map/pallas_call | solution.py:468
